TPU v7x, 128 devices: a whole 4x4x4 slice. The times are simulated.
128 devices in a mesh: rep: 2 (over core), dp: 64 (over x, y, z).
Axes of the slice: x: 4, y: 4, z: 4, core: 2. Of those that a mesh axis runs over, the one named last changes fastest.
Arguments:
- x: bfloat16 [128, 2048, 1280], P(('rep', 'dp')), parts along dimension 0
- dy: bfloat16 [128, 2048, 1280], P(('rep', 'dp')), parts along dimension 0
- w_gate: bfloat16 [2, 1280, 3072], P(None, 'dp')
- w_up: bfloat16 [2, 1280, 3072], P(None, 'dp')
- w_down: bfloat16 [2, 3072, 1280], P(None, 'dp')
Outputs:
- output 1: bfloat16 [128, 2048, 1280], P(('rep', 'dp')), parts along dimension 0
- output 2: bfloat16 [4, 1280, 3072], P('rep', 'dp'), parts along dimension 0
- output 3: bfloat16 [4, 1280, 3072], P('rep', 'dp'), parts along dimension 0
- output 4: bfloat16 [4, 3072, 1280], P('rep', 'dp'), parts along dimension 0
There are 2 independent parts. A program takes and returns all parts, laid end to end along the dimension named above; an argument that names none is the same for every part.
All inputs are finite; a program needn't handle non-finite values.
Results may differ from a plain program's by a relative error of at most 0.018.
Values are sent between devices in bfloat16 or wider.
A program may use at most 1.5 GiB of HBM per device.

v0:
```python
import jax
import jax.numpy as jnp
from jax import lax

NAMES = ("w_gate", "w_up", "w_down")


def matmul(a, w):
    return jnp.dot(a, w, preferred_element_type=jnp.float32).astype(jnp.bfloat16)


def normed(h):
    wide = h.astype(jnp.float32)
    scale = lax.rsqrt(jnp.mean(wide**2, -1, keepdims=True) + 1e-6)
    return (wide * scale).astype(jnp.bfloat16)


def layer(h, w):
    a = normed(h)
    gate = jnp.dot(a, w["w_gate"], preferred_element_type=jnp.float32)
    up = jnp.dot(a, w["w_up"], preferred_element_type=jnp.float32)
    return h + matmul((jax.nn.silu(gate) * up).astype(jnp.bfloat16), w["w_down"])


def stack(weights, h):
    for number in range(weights["w_gate"].shape[0]):
        h = layer(h, {name: w[number] for name, w in weights.items()})
    return h


def solution(mesh):
    groups = mesh.shape["rep"]

    def step(x, dy, *weights):
        shape = x.shape
        x, dy = (t.reshape(groups, -1, *t.shape[1:]) for t in (x, dy))

        def of_a_group(x, dy):
            _, back = jax.vjp(stack, dict(zip(NAMES, weights, strict=True)), x)
            by_weights, by_x = back(dy)
            return (by_x, *(by_weights[name] for name in NAMES))

        by_x, *by_weights = jax.vmap(of_a_group)(x, dy)
        return (by_x.reshape(shape), *(t.reshape(-1, *t.shape[2:]) for t in by_weights))

    return step
```

profile of v0, /device:TPU:0, one launch (start us, length us, event | category | flops | bytes accessed | tf_op | source)
XLA Modules:
  0.0 2134.7 jit_solution(4685541190715141298)
XLA Ops:
  19.0 7.9 copy.15
  27.4 7.9 copy.14
  35.4 79.0 %all-gather.31.cloned.1.call-done = bf16[1,1280,3072]{2,0,1:T(2,128)(2,1)} async-done(((bf16[1,20,3072]{2,0,1:T(2,128)(2,1)}), bf16[1,1280,3072]{2,0,1:T(2,128)(2,1)}) %all-gather.31.cloned.1.call-update) | async-done | bytes 7864336 | tf_op jit(solution)/vmap(jvp())/squeeze | solution.py:27
  114.4 24.9 %fusion.60 = f32[2048,3072]{1,0:T(8,128)} fusion(bf16[1,1280,3072]{2,0,1:T(2,128)(2,1)} %all-gather.31.cloned.1.call-done, bf16[1,2048,1280]{2,1,0:T(8,128)(2,1)} %param.1, f32[2048]{0:T(1024)S(1)} %get-tuple-element.69), kind=kOutput, calls=%fused_computation.78 | convolution fusion | flops 16113991680 | bytes 38281216 | tf_op jit(solution)/vmap(jvp())/dot_general | solution.py:21
  139.3 77.9 %all-gather.29.cloned.1.call-done = bf16[1,1280,3072]{2,0,1:T(2,128)(2,1)} async-done(((bf16[1,20,3072]{2,0,1:T(2,128)(2,1)}), bf16[1,1280,3072]{2,0,1:T(2,128)(2,1)}) %all-gather.29.cloned.1.call-update) | async-done | bytes 7864336 | tf_op jit(solution)/vmap(jvp())/squeeze | solution.py:27
  217.2 25.0 %fusion.64 = f32[2048,3072]{1,0:T(8,128)} fusion(bf16[1,1280,3072]{2,0,1:T(2,128)(2,1)} %all-gather.29.cloned.1.call-done, bf16[1,2048,1280]{2,1,0:T(8,128)(2,1)} %param.1, f32[2048]{0:T(1024)S(1)} %get-tuple-element.69), kind=kOutput, calls=%fused_computation.82 | convolution fusion | flops 16113991680 | bytes 38281216 | tf_op jit(solution)/vmap(jvp())/dot_general | solution.py:20
  242.2 21.7 %fusion.34 = bf16[2048,3072]{1,0:T(8,128)(2,1)} fusion(f32[2048,3072]{1,0:T(8,128)} %fusion.60, f32[2048,3072]{1,0:T(8,128)} %fusion.64), kind=kLoop, calls=%fused_computation.51 | loop fusion | flops 37748736 | bytes 62914560
  263.9 31.9 %all-gather.33.cloned.1.call-done = bf16[1,3072,1280]{2,1,0:T(8,128)(2,1)} async-done(((bf16[1,48,1280]{2,1,0:T(8,128)(2,1)}), bf16[1,3072,1280]{2,1,0:T(8,128)(2,1)}) %all-gather.33.cloned.1.call-update) | async-done | bytes 7864336 | tf_op jit(solution)/vmap(jvp())/squeeze | solution.py:27
  295.8 23.6 %fusion.49 = (f32[2048]{0:T(1024)S(1)}, bf16[1,1,2048,1280]{2,3,1,0:T(8,128)(2,1)}) fusion(bf16[2048,3072]{1,0:T(8,128)(2,1)} %fusion.34, bf16[1,3072,1280]{2,1,0:T(8,128)(2,1)} %all-gather.33.cloned.1.call-done, bf16[1,2048,1280]{1,2,0:T(8,128)(2,1)} %copy.15), kind=kOutput, calls=%fused_computation.67 | convolution fusion | flops 16119232512 | bytes 30941184 | tf_op jit(solution)/vmap(jvp())/dot_general | solution.py:9
  320.1 54.2 %all-gather.37.cloned.1.call-done = bf16[1,3072,1280]{2,1,0:T(8,128)(2,1)} async-done(((bf16[1,48,1280]{2,1,0:T(8,128)(2,1)}), bf16[1,3072,1280]{2,1,0:T(8,128)(2,1)}) %all-gather.37.cloned.1.call-update) | async-done | bytes 7864336 | tf_op jit(solution)/vmap(jvp())/squeeze | solution.py:27
  374.3 22.7 %convolution_convert_fusion.1 = bf16[2048,3072]{1,0:T(8,128)(2,1)} fusion(bf16[1,3072,1280]{2,1,0:T(8,128)(2,1)} %all-gather.37.cloned.1.call-done, bf16[1,2048,1280]{2,1,0:T(8,128)(2,1)} %param), kind=kOutput, calls=%fused_computation.58 | convolution fusion | flops 16112418816 | bytes 25690112 | tf_op jit(solution)/vmap(transpose(jvp()))/dot_general | solution.py:9
  396.9 80.6 %all-gather.35.cloned.1.call-done = bf16[1,1280,3072]{2,0,1:T(2,128)(2,1)} async-done(((bf16[1,20,3072]{2,0,1:T(2,128)(2,1)}), bf16[1,1280,3072]{2,0,1:T(2,128)(2,1)}) %all-gather.35.cloned.1.call-update) | async-done | bytes 7864336 | tf_op jit(solution)/vmap(jvp())/squeeze | solution.py:27
  477.5 25.3 %fusion.57 = f32[2048,3072]{1,0:T(8,128)} fusion(bf16[1,1,2048,1280]{2,3,1,0:T(8,128)(2,1)} %get-tuple-element.71, f32[2048]{0:T(1024)S(1)} %bitcast.320, bf16[1,1280,3072]{2,0,1:T(2,128)(2,1)} %all-gather.35.cloned.1.call-done), kind=kOutput, calls=%fused_computation.75 | convolution fusion | flops 16113991680 | bytes 38281216 | tf_op jit(solution)/vmap(jvp())/dot_general | solution.py:20
  502.8 78.0 %all-gather.39.cloned.1.call-done = bf16[1,1280,3072]{2,0,1:T(2,128)(2,1)} async-done(((bf16[1,20,3072]{2,0,1:T(2,128)(2,1)}), bf16[1,1280,3072]{2,0,1:T(2,128)(2,1)}) %all-gather.39.cloned.1.call-update) | async-done | bytes 7864336 | tf_op jit(solution)/vmap(jvp())/squeeze | solution.py:27
  580.8 25.5 %fusion.52 = f32[2048,3072]{1,0:T(8,128)} fusion(bf16[1,1,2048,1280]{2,3,1,0:T(8,128)(2,1)} %get-tuple-element.71, f32[2048]{0:T(1024)S(1)} %bitcast.321, bf16[1,1280,3072]{2,0,1:T(2,128)(2,1)} %all-gather.39.cloned.1.call-done), kind=kOutput, calls=%fused_computation.70 | convolution fusion | flops 16113991680 | bytes 38281216 | tf_op jit(solution)/vmap(jvp())/dot_general | solution.py:21
  606.4 22.7 %fusion.8 = bf16[2048,3072]{1,0:T(8,128)(2,1)} fusion(f32[2048,3072]{1,0:T(8,128)} %fusion.57, f32[2048,3072]{1,0:T(8,128)} %fusion.52, bf16[2048,3072]{1,0:T(8,128)(2,1)S(1)} %copy-done), kind=kLoop, calls=%fused_computation.10 | loop fusion | flops 75497472 | bytes 75497472
  629.1 27.9 %fusion.79 = bf16[2048,1280]{0,1:T(8,128)(2,1)} fusion(bf16[2048,3072]{1,0:T(8,128)(2,1)} %convolution_convert_fusion.1, f32[2048,3072]{1,0:T(8,128)} %fusion.57, bf16[1,1280,3072]{2,0,1:T(2,128)(2,1)} %all-gather.39.cloned.1.call-done), kind=kOutput, calls=%fused_computation.91 | convolution fusion | flops 16146497536 | bytes 50855936 | tf_op jit(solution)/vmap(transpose(jvp()))/dot_general | solution.py:21
  657.0 28.7 %fusion.51 = (f32[2048]{0:T(1024)S(1)}, bf16[1,1,2048,1280]{2,3,1,0:T(8,128)(2,1)}) fusion(bf16[1,1,2048,1280]{2,3,1,0:T(8,128)(2,1)} %get-tuple-element.71, bf16[2048,1280]{0,1:T(8,128)(2,1)} %fusion.79, bf16[2048,3072]{1,0:T(8,128)(2,1)} %fusion.8, bf16[1,1280,3072]{2,0,1:T(2,128)(2,1)} %all-gather.35.cloned.1.call-done), kind=kOutput, calls=%fused_computation.69 | convolution fusion | flops 16119232512 | bytes 36184064 | tf_op jit(solution)/vmap(transpose(jvp()))/dot_general | solution.py:20
  685.8 12.3 fusion.111
  698.1 22.5 %convolution_bitcast_fusion = f32[1,3072,1280]{2,1,0:T(8,128)} fusion(bf16[2048,3072]{1,0:T(8,128)(2,1)} %fusion.34, bf16[1,1,2048,1280]{2,3,1,0:T(8,128)(2,1)} %fusion.111), kind=kOutput, calls=%fused_computation.47 | convolution fusion | flops 16106127360 | bytes 33554432 | tf_op jit(solution)/vmap(transpose(jvp()))/dot_general | solution.py:9
  720.6 20.7 convolution_convert_fusion
  741.3 4.6 copy-done.1
  745.9 22.9 %fusion.11 = bf16[2048,3072]{1,0:T(8,128)(2,1)} fusion(f32[2048,3072]{1,0:T(8,128)} %fusion.64, f32[2048,3072]{1,0:T(8,128)} %fusion.60, bf16[2048,3072]{1,0:T(8,128)(2,1)S(1)} %convolution_convert_fusion), kind=kLoop, calls=%fused_computation.13 | loop fusion | flops 75497472 | bytes 75497472
  768.9 28.0 %fusion.84 = bf16[2048,1280]{0,1:T(8,128)(2,1)} fusion(bf16[2048,3072]{1,0:T(8,128)(2,1)} %copy-done.1, f32[2048,3072]{1,0:T(8,128)} %fusion.64, bf16[1,1280,3072]{2,0,1:T(2,128)(2,1)} %all-gather.31.cloned.1.call-done), kind=kOutput, calls=%fused_computation.92 | convolution fusion | flops 16146497536 | bytes 50855936 | tf_op jit(solution)/vmap(transpose(jvp()))/dot_general | solution.py:21
  796.9 28.5 %fusion.47 = (f32[2048]{0:T(1024)S(1)}, bf16[1,1,2048,1280]{2,3,1,0:T(8,128)(2,1)}) fusion(bf16[1,2048,1280]{1,2,0:T(8,128)(2,1)} %copy.15, bf16[2048,1280]{0,1:T(8,128)(2,1)} %fusion.84, bf16[2048,3072]{1,0:T(8,128)(2,1)} %fusion.11, bf16[1,1280,3072]{2,0,1:T(2,128)(2,1)} %all-gather.29.cloned.1.call-done), kind=kOutput, calls=%fused_computation.65 | convolution fusion | flops 16119232512 | bytes 36184064 | tf_op jit(solution)/vmap(transpose(jvp()))/dot_general | solution.py:20
  826.1 23.0 %convolution_bitcast_fusion.3 = f32[1,1280,3072]{2,1,0:T(8,128)} fusion(bf16[2048,3072]{1,0:T(8,128)(2,1)} %fusion.8, bf16[1,1,2048,1280]{2,3,1,0:T(8,128)(2,1)} %get-tuple-element.71, f32[2048]{0:T(1024)S(1)} %bitcast.323), kind=kOutput, calls=%fused_computation.50 | convolution fusion | flops 16113991680 | bytes 33562624 | tf_op jit(solution)/vmap(transpose(jvp()))/dot_general | solution.py:20
  849.1 21.0 convolution_bitcast_fusion.2
  870.1 30.7 %convolution_bitcast_fusion.1 = f32[1,3072,1280]{2,1,0:T(8,128)} fusion(f32[2048,3072]{1,0:T(8,128)} %fusion.52, f32[2048,3072]{1,0:T(8,128)} %fusion.57, bf16[1,2048,1280]{2,1,0:T(8,128)(2,1)} %param), kind=kOutput, calls=%fused_computation.48 | convolution fusion | flops 16143876096 | bytes 71303168 | tf_op jit(solution)/vmap(transpose(jvp()))/dot_general | solution.py:9
  900.8 434.9 %fusion.143 = (f32[24,3072]{1,0:T(8,128)S(1)}, f32[24,3072]{1,0:T(8,128)S(1)}) fusion(f32[1,1280,3072]{2,1,0:T(8,128)} %convolution_bitcast_fusion.2, f32[1,1280,3072]{2,1,0:T(8,128)} %convolution_bitcast_fusion.3), kind=kCustom, calls=%all-reduce-scatter.4 | all-reduce-scatter fusion | flops 9437185 | bytes 32047616
  1335.7 26.9 %fusion.31 = f32[1,1280,3072]{2,1,0:T(8,128)} fusion(bf16[2048,3072]{1,0:T(8,128)(2,1)} %copy-done.1, f32[2048,3072]{1,0:T(8,128)} %fusion.64, bf16[1,2048,1280]{1,2,0:T(8,128)(2,1)} %copy.15, f32[2048]{0:T(1024)S(1)} %bitcast.326), kind=kOutput, calls=%fused_computation.46 | convolution fusion | flops 16151740416 | bytes 58728448 | tf_op jit(solution)/vmap(transpose(jvp()))/dot_general | solution.py:21
  1366.1 25.3 %fusion.28 = f32[1,1280,3072]{2,1,0:T(8,128)} fusion(bf16[2048,3072]{1,0:T(8,128)(2,1)} %convolution_convert_fusion.1, f32[2048,3072]{1,0:T(8,128)} %fusion.57, bf16[1,1,2048,1280]{2,3,1,0:T(8,128)(2,1)S(1)} %bitcast.316, f32[2048]{0:T(1024)S(1)} %bitcast.324), kind=kOutput, calls=%fused_computation.45 | convolution fusion | flops 16151740416 | bytes 58728448 | tf_op jit(solution)/vmap(transpose(jvp()))/dot_general | solution.py:21
  1391.4 449.7 %fusion.144 = (f32[24,3072]{1,0:T(8,128)S(1)}, f32[24,3072]{1,0:T(8,128)S(1)}) fusion(f32[1,1280,3072]{2,1,0:T(8,128)} %fusion.31, f32[1,1280,3072]{2,1,0:T(8,128)} %fusion.28), kind=kCustom, calls=%all-reduce-scatter.5 | all-reduce-scatter fusion | flops 9437185 | bytes 32047616
  1845.4 8.3 collective-permute-start.20
  1857.5 5.7 collective-permute-start.17
  1871.0 8.2 collective-permute-start.13
  1884.6 7.8 collective-permute-start.9
  1899.9 7.2 collective-permute-start.5
  1911.0 8.9 collective-permute-start.2
  1940.3 12.3 fusion.110
  1953.3 7.9 copy.16
  1961.1 32.7 %concatenate.1 = bf16[276,3072]{1,0:T(8,128)(2,1)} concatenate(bf16[12,3072]{1,0:T(8,128)(2,1)} %copy-done.17, bf16[24,3072]{1,0:T(8,128)(2,1)S(1)} %collective-permute-done.20, bf16[24,3072]{1,0:T(8,128)(2,1)S(1)} %collective-permute-done.19, bf16[24,3072]{1,0:T(8,128)(2,1)S(1)} %collective-permute-done.18, bf16[24,3072]{1,0:T(8,128)(2,1)S(1)} %collective-permute-done.17, ...), dimensions={0} | concatenate | bytes 3538944
  1999.0 6.6 collective-permute-start.35
  2005.5 4.9 collective-permute-start.34
  2012.7 33.2 %concatenate = bf16[276,3072]{1,0:T(8,128)(2,1)} concatenate(bf16[12,3072]{1,0:T(8,128)(2,1)} %copy-done.16, bf16[24,3072]{1,0:T(8,128)(2,1)S(1)} %collective-permute-done.9, bf16[24,3072]{1,0:T(8,128)(2,1)S(1)} %collective-permute-done.8, bf16[24,3072]{1,0:T(8,128)(2,1)S(1)} %collective-permute-done.7, bf16[24,3072]{1,0:T(8,128)(2,1)S(1)} %collective-permute-done.6, ...), dimensions={0} | concatenate | bytes 3538944
  2045.9 5.2 collective-permute-start.31
  2067.7 5.3 collective-permute-start.24
  2080.3 8.9 concatenate.3
  2089.2 33.7 %concatenate.2 = bf16[276,3072]{1,0:T(8,128)(2,1)} concatenate(bf16[12,3072]{1,0:T(8,128)(2,1)} %copy-done.15, bf16[24,3072]{1,0:T(8,128)(2,1)S(1)} %collective-permute-done.31, bf16[24,3072]{1,0:T(8,128)(2,1)} %copy-done.11, bf16[24,3072]{1,0:T(8,128)(2,1)} %copy-done.12, bf16[24,3072]{1,0:T(8,128)(2,1)} %copy-done.13, bf16[24,3072]{1,0:T(8,128)(2,1)} %copy-done.14, ...), dimensions={0} | concatenate | bytes 3538944
  (184 shorter events, 105.5 us)
Async XLA Ops:
  7.2 107.2 %all-gather.31.cloned.1.call-start = ((), (), s32[]{:S(2)}) async-start(), calls=%async_computation.3 | async-start | bytes 15974400 | tf_op jit(solution)/vmap(jvp())/squeeze | solution.py:27
  9.5 207.7 %all-gather.29.cloned.1.call-start = ((), (), s32[]{:S(2)}) async-start(), calls=%async_computation.2 | async-start | bytes 15974400 | tf_op jit(solution)/vmap(jvp())/squeeze | solution.py:27
  11.8 284.0 %all-gather.33.cloned.1.call-start = ((), (), s32[]{:S(2)}) async-start(), calls=%async_computation.4 | async-start | bytes 7987200 | tf_op jit(solution)/vmap(jvp())/squeeze | solution.py:27
  13.6 360.7 %all-gather.37.cloned.1.call-start = ((), (), s32[]{:S(2)}) async-start(), calls=%async_computation.6 | async-start | bytes 7987200 | tf_op jit(solution)/vmap(jvp())/squeeze | solution.py:27
  14.2 463.4 %all-gather.35.cloned.1.call-start = ((), (), s32[]{:S(2)}) async-start(), calls=%async_computation.5 | async-start | bytes 15974400 | tf_op jit(solution)/vmap(jvp())/squeeze | solution.py:27
  14.8 566.1 %all-gather.39.cloned.1.call-start = ((), (), s32[]{:S(2)}) async-start(), calls=%async_computation.7 | async-start | bytes 15974400 | tf_op jit(solution)/vmap(jvp())/squeeze | solution.py:27
  15.3 2109.6 %reduce-scatter.25.cloned.1.call-start = ((), (), s32[]{:S(2)}) async-start(), calls=%async_computation.9 | async-start | bytes 15974400
  768.8 1357.1 %reduce-scatter.23.cloned.1.call-start = ((), (), s32[]{:S(2)}) async-start(), calls=%async_computation.8 | async-start | bytes 15974400
  1362.6 491.1 %collective-permute-start.21 = (bf16[12,3072]{1,0:T(8,128)(2,1)S(1)}, bf16[12,3072]{1,0:T(8,128)(2,1)S(1)}, u32[]{:S(2)}, u32[]{:S(2)}) collective-permute-start(bf16[12,3072]{1,0:T(8,128)(2,1)S(1)} %slice.25), channel_id=1, source_target_pairs={{0,11},{1,12},{2,13},{3,14},{4,15},{5,16},{6,17},{7,18},{8,19},{9,... | collective-permute-start | bytes 221192
  1363.9 491.1 %collective-permute-start.10 = (bf16[12,3072]{1,0:T(8,128)(2,1)S(1)}, bf16[12,3072]{1,0:T(8,128)(2,1)S(1)}, u32[]{:S(2)}, u32[]{:S(2)}) collective-permute-start(bf16[12,3072]{1,0:T(8,128)(2,1)S(1)} %slice.24), channel_id=1, source_target_pairs={{0,11},{1,12},{2,13},{3,14},{4,15},{5,16},{6,17},{7,18},{8,19},{9,... | collective-permute-start | bytes 221192
  1841.1 16.3 collective-permute-start.43
  1843.1 20.1 collective-permute-start.32
  1845.4 19.1 collective-permute-start.20
  1853.7 15.2 collective-permute-start.19
  1855.0 16.0 collective-permute-start.18
  1857.5 21.7 %collective-permute-start.17 = (bf16[24,3072]{1,0:T(8,128)(2,1)S(1)}, bf16[24,3072]{1,0:T(8,128)(2,1)S(1)}, u32[]{:S(2)}, u32[]{:S(2)}) collective-permute-start(bf16[24,3072]{1,0:T(8,128)(2,1)S(1)} %convert.136), channel_id=1, source_target_pairs={{0,7},{1,8},{2,9},{3,10},{4,11},{5,12},{6,13},{7,14},{8,15},{9,16}... | collective-permute-start | bytes 442376
  1863.2 17.3 collective-permute-start.16
  1864.5 20.1 collective-permute-start.15
  1868.9 23.6 %collective-permute-start.14 = (bf16[24,3072]{1,0:T(8,128)(2,1)S(1)}, bf16[24,3072]{1,0:T(8,128)(2,1)S(1)}, u32[]{:S(2)}, u32[]{:S(2)}) collective-permute-start(bf16[24,3072]{1,0:T(8,128)(2,1)S(1)} %convert.136), channel_id=1, source_target_pairs={{0,4},{1,5},{2,6},{3,7},{4,8},{5,9},{6,10},{7,11},{8,12},{9,13},{1... | collective-permute-start | bytes 442376
  1871.0 22.7 %collective-permute-start.13 = (bf16[24,3072]{1,0:T(8,128)(2,1)S(1)}, bf16[24,3072]{1,0:T(8,128)(2,1)}, u32[]{:S(2)}, u32[]{:S(2)}) collective-permute-start(bf16[24,3072]{1,0:T(8,128)(2,1)S(1)} %convert.136), channel_id=1, source_target_pairs={{0,3},{1,4},{2,5},{3,6},{4,7},{5,8},{6,9},{7,10},{8,11},{9,12},{10... | collective-permute-start | bytes 442376
  1879.2 19.2 collective-permute-start.12
  1880.5 19.3 collective-permute-start.11
  1884.6 22.5 %collective-permute-start.9 = (bf16[24,3072]{1,0:T(8,128)(2,1)}, bf16[24,3072]{1,0:T(8,128)(2,1)S(1)}, u32[]{:S(2)}, u32[]{:S(2)}) collective-permute-start(bf16[24,3072]{1,0:T(8,128)(2,1)} %convert.135), channel_id=1, source_target_pairs={{0,10},{1,11},{2,12},{3,13},{4,14},{5,15},{6,16},{7,17},{8,18},{9,... | collective-permute-start | bytes 442376
  1892.4 16.0 collective-permute-start.8
  1893.8 17.2 collective-permute-start.7
  1898.4 21.5 %collective-permute-start.6 = (bf16[24,3072]{1,0:T(8,128)(2,1)}, bf16[24,3072]{1,0:T(8,128)(2,1)S(1)}, u32[]{:S(2)}, u32[]{:S(2)}) collective-permute-start(bf16[24,3072]{1,0:T(8,128)(2,1)} %convert.135), channel_id=1, source_target_pairs={{0,7},{1,8},{2,9},{3,10},{4,11},{5,12},{6,13},{7,14},{8,15},{9,16}... | collective-permute-start | bytes 442376
  1899.9 21.4 %collective-permute-start.5 = (bf16[24,3072]{1,0:T(8,128)(2,1)}, bf16[24,3072]{1,0:T(8,128)(2,1)S(1)}, u32[]{:S(2)}, u32[]{:S(2)}) collective-permute-start(bf16[24,3072]{1,0:T(8,128)(2,1)} %convert.135), channel_id=1, source_target_pairs={{0,6},{1,7},{2,8},{3,9},{4,10},{5,11},{6,12},{7,13},{8,14},{9,15},... | collective-permute-start | bytes 442376
  1907.2 20.7 collective-permute-start.4
  1908.5 21.2 collective-permute-start.3
  1911.0 20.5 collective-permute-start.2
  1921.3 15.2 collective-permute-start
  1927.9 65.9 %collective-permute-start.42 = (bf16[24,3072]{1,0:T(8,128)(2,1)}, bf16[24,3072]{1,0:T(8,128)(2,1)S(1)}, u32[]{:S(2)}, u32[]{:S(2)}) collective-permute-start(bf16[24,3072]{1,0:T(8,128)(2,1)} %convert.134), channel_id=1, source_target_pairs={{0,10},{1,11},{2,12},{3,13},{4,14},{5,15},{6,16},{7,17},{8,18},{9,... | collective-permute-start | bytes 442376
  1929.7 67.3 %collective-permute-start.41 = (bf16[24,3072]{1,0:T(8,128)(2,1)}, bf16[24,3072]{1,0:T(8,128)(2,1)S(1)}, u32[]{:S(2)}, u32[]{:S(2)}) collective-permute-start(bf16[24,3072]{1,0:T(8,128)(2,1)} %convert.134), channel_id=1, source_target_pairs={{0,9},{1,10},{2,11},{3,12},{4,13},{5,14},{6,15},{7,16},{8,17},{9,1... | collective-permute-start | bytes 442376
  1931.5 67.4 %collective-permute-start.40 = (bf16[24,3072]{1,0:T(8,128)(2,1)}, bf16[24,3072]{1,0:T(8,128)(2,1)S(1)}, u32[]{:S(2)}, u32[]{:S(2)}) collective-permute-start(bf16[24,3072]{1,0:T(8,128)(2,1)} %convert.134), channel_id=1, source_target_pairs={{0,8},{1,9},{2,10},{3,11},{4,12},{5,13},{6,14},{7,15},{8,16},{9,17... | collective-permute-start | bytes 442376
  1934.9 70.6 %collective-permute-start.39 = (bf16[24,3072]{1,0:T(8,128)(2,1)}, bf16[24,3072]{1,0:T(8,128)(2,1)S(1)}, u32[]{:S(2)}, u32[]{:S(2)}) collective-permute-start(bf16[24,3072]{1,0:T(8,128)(2,1)} %convert.134), channel_id=1, source_target_pairs={{0,7},{1,8},{2,9},{3,10},{4,11},{5,12},{6,13},{7,14},{8,15},{9,16}... | collective-permute-start | bytes 442376
  1936.5 73.9 %collective-permute-start.38 = (bf16[24,3072]{1,0:T(8,128)(2,1)}, bf16[24,3072]{1,0:T(8,128)(2,1)S(1)}, u32[]{:S(2)}, u32[]{:S(2)}) collective-permute-start(bf16[24,3072]{1,0:T(8,128)(2,1)} %convert.134), channel_id=1, source_target_pairs={{0,6},{1,7},{2,8},{3,9},{4,10},{5,11},{6,12},{7,13},{8,14},{9,15},... | collective-permute-start | bytes 442376
  1993.8 52.1 %collective-permute-start.37 = (bf16[24,3072]{1,0:T(8,128)(2,1)}, bf16[24,3072]{1,0:T(8,128)(2,1)S(1)}, u32[]{:S(2)}, u32[]{:S(2)}) collective-permute-start(bf16[24,3072]{1,0:T(8,128)(2,1)} %convert.134), channel_id=1, source_target_pairs={{0,5},{1,6},{2,7},{3,8},{4,9},{5,10},{6,11},{7,12},{8,13},{9,14},{... | collective-permute-start | bytes 442376
  1997.0 54.1 %collective-permute-start.36 = (bf16[24,3072]{1,0:T(8,128)(2,1)}, bf16[24,3072]{1,0:T(8,128)(2,1)S(1)}, u32[]{:S(2)}, u32[]{:S(2)}) collective-permute-start(bf16[24,3072]{1,0:T(8,128)(2,1)} %convert.134), channel_id=1, source_target_pairs={{0,4},{1,5},{2,6},{3,7},{4,8},{5,9},{6,10},{7,11},{8,12},{9,13},{1... | collective-permute-start | bytes 442376
  1999.0 53.8 %collective-permute-start.35 = (bf16[24,3072]{1,0:T(8,128)(2,1)}, bf16[24,3072]{1,0:T(8,128)(2,1)S(1)}, u32[]{:S(2)}, u32[]{:S(2)}) collective-permute-start(bf16[24,3072]{1,0:T(8,128)(2,1)} %convert.134), channel_id=1, source_target_pairs={{0,3},{1,4},{2,5},{3,6},{4,7},{5,8},{6,9},{7,10},{8,11},{9,12},{10... | collective-permute-start | bytes 442376
  2005.5 48.6 %collective-permute-start.34 = (bf16[24,3072]{1,0:T(8,128)(2,1)}, bf16[24,3072]{1,0:T(8,128)(2,1)S(1)}, u32[]{:S(2)}, u32[]{:S(2)}) collective-permute-start(bf16[24,3072]{1,0:T(8,128)(2,1)} %convert.134), channel_id=1, source_target_pairs={{0,2},{1,3},{2,4},{3,5},{4,6},{5,7},{6,8},{7,9},{8,10},{9,11},{10,... | collective-permute-start | bytes 442376
  2010.4 46.9 %collective-permute-start.33 = (bf16[24,3072]{1,0:T(8,128)(2,1)}, bf16[24,3072]{1,0:T(8,128)(2,1)S(1)}, u32[]{:S(2)}, u32[]{:S(2)}) collective-permute-start(bf16[24,3072]{1,0:T(8,128)(2,1)} %convert.134), channel_id=1, source_target_pairs={{0,1},{1,2},{2,3},{3,4},{4,5},{5,6},{6,7},{7,8},{8,9},{9,10},{10,1... | collective-permute-start | bytes 442376
  2045.9 16.7 collective-permute-start.31
  2054.1 18.9 collective-permute-start.28
  2057.3 17.6 collective-permute-start.27
  2062.6 26.6 %collective-permute-start.26 = (bf16[24,3072]{1,0:T(8,128)(2,1)}, bf16[24,3072]{1,0:T(8,128)(2,1)}, u32[]{:S(2)}, u32[]{:S(2)}) collective-permute-start(bf16[24,3072]{1,0:T(8,128)(2,1)} %convert.133), channel_id=1, source_target_pairs={{0,5},{1,6},{2,7},{3,8},{4,9},{5,10},{6,11},{7,12},{8,13},{9,14},{... | collective-permute-start | bytes 442376
  2064.6 24.6 %collective-permute-start.25 = (bf16[24,3072]{1,0:T(8,128)(2,1)}, bf16[24,3072]{1,0:T(8,128)(2,1)}, u32[]{:S(2)}, u32[]{:S(2)}) collective-permute-start(bf16[24,3072]{1,0:T(8,128)(2,1)} %convert.133), channel_id=1, source_target_pairs={{0,4},{1,5},{2,6},{3,7},{4,8},{5,9},{6,10},{7,11},{8,12},{9,13},{1... | collective-permute-start | bytes 442376
  2067.7 21.5 %collective-permute-start.24 = (bf16[24,3072]{1,0:T(8,128)(2,1)}, bf16[24,3072]{1,0:T(8,128)(2,1)}, u32[]{:S(2)}, u32[]{:S(2)}) collective-permute-start(bf16[24,3072]{1,0:T(8,128)(2,1)} %convert.133), channel_id=1, source_target_pairs={{0,3},{1,4},{2,5},{3,6},{4,7},{5,8},{6,9},{7,10},{8,11},{9,12},{10... | collective-permute-start | bytes 442376
  2073.0 16.2 collective-permute-start.23
  (33 other events, 1588.8 us)
Sparse Core Ops, SparseCore 0:
  11.4 102.9 all-gather.30
  117.2 99.9 all-gather.28
  220.1 75.6 all-gather.32
  298.5 75.6 all-gather.36
  377.5 99.9 all-gather.34
  480.8 99.9 all-gather.38
  768.9 582.3 reduce-scatter.24
  1356.0 553.3 reduce-scatter.22
where the time goes:
time: 2150 us; the launch traced here: 2130 us
  blocking collectives  885 us (41%)
  matrix products  430 us (20%)
  waiting for transfers between devices  403 us (19%)
  local copies, waits for them, and re-layouts  150 us (7%)
  starting transfers between devices  149 us (7%)
  other arithmetic  102 us (5%)
    unnamed x2, blocking collectives  885 us
    squeeze x6, waiting for transfers between devices, stack(): h = layer(h, {name: w[number] for name, w in weights.items()})  402 us
    dot_general x6, matrix products, layer(): up = jnp.dot(a, w['w_up'], preferred_element_type=jnp.float32)  158 us
    dot_general x6, matrix products, layer(): gate = jnp.dot(a, w['w_gate'], preferred_element_type=jnp.float32)  151 us
    unnamed x46, starting transfers between devices  149 us
    unnamed x72, local copies, waits for them, and re-layouts  141 us
    dot_general x5, matrix products, matmul(): jnp.dot(a, w, preferred_element_type=jnp.float32).astype(jnp.bfloat16)  120 us
    unnamed x9, other arithmetic  69.4 us
  transfers between devices with their start and end apart: 52, of which 6 were waited for; matrix products, arithmetic and copies ran while one was open for 64% of the time, Pallas kernels for 0%

commit v1 on v0

v1 whole, which is shorter than its diff:
```python
import jax
import jax.numpy as jnp
from jax import lax
from jax.experimental import pallas as pl
from jax.experimental.pallas import tpu as pltpu
from jax.sharding import PartitionSpec as P

MESH = pl.DeviceIdType.MESH
BF = jnp.bfloat16
F32 = jnp.float32
L, D, FF, T = 2, 1280, 3072, 2048
RING = 4
ROWS = D // 64
JOINED = RING * ROWS
DROWS = FF // 64
CH = 512
HC = CH // 2
NJ = FF // CH
UNITS = L * NJ
MXU = 256
ND = D // MXU
ALL = slice(None)
HALVES = (lambda: ALL, lambda: pl.ds(0, 2), lambda: pl.ds(2, 2))
NN = (((1,), (0,)), ((), ()))
NT = (((1,), (1,)), ((), ()))
LANES = 128


def dot(a, b, dims=NN):
    return lax.dot_general(a, b, dims, preferred_element_type=F32)


def local(src, dst, sem):
    return pltpu.make_async_copy(src, dst, sem)


def remote(src, dst, send, recv, device):
    return pltpu.make_async_remote_copy(src_ref=src, dst_ref=dst, send_sem=send, recv_sem=recv, device_id=device, device_id_type=MESH)


def aligned(start, size):
    return pl.ds(pl.multiple_of(start, LANES), size)


def piece(index, size):
    return aligned(index * size, size)


def mod(a, n):
    return lax.rem(a, n)


def div(a, n):
    return lax.div(a, n)


class Place:
    def __init__(self):
        self.core = lax.axis_index("rep")
        self.dp = lax.axis_index("dp")
        self.other = 1 - self.core
        self.place, self.device = {}, {}
        for stride, axis in ((RING**2, "x"), (RING, "y"), (1, "z")):
            at = mod(div(self.dp, stride), RING)
            for by in range(RING):
                self.place[axis, by] = mod(at + by, RING)
                self.device[axis, by] = (self.core, self.dp + (self.place[axis, by] - at) * stride)

    def to(self, axis, by):
        return self.device[axis, by % RING]

    def index(self, axis, by=0):
        return self.place[axis, by % RING]

    def partner(self):
        return (self.other, self.dp)

    def greet(self, others):
        barrier = pltpu.get_barrier_semaphore()
        for other in others:
            pl.semaphore_signal(barrier, inc=1, device_id=other, device_id_type=MESH)
        pl.semaphore_wait(barrier, len(others))


class Gather:
    def __init__(self, place, full, own, send, recv):
        self.p, self.full, self.own, self.send, self.recv = place, full, own, send, recv

    def ring(self, axis, ref, parts, receive):
        s, r = (-1, 1) if receive else (0, 0)
        whole, low, high = parts
        right, left = self.p.to(axis, 1), self.p.to(axis, -1)
        return [(lambda: ref(s, whole()), right), (lambda: ref(r, whole()), left), (lambda: ref(s - 1, low()), right), (lambda: ref(r + 1, high()), left)]

    def hand(self, ref):
        return [(lambda by=by: ref(by), self.p.partner()) for by in (0, -1, 1, 2)]

    def copy(self, k, u, receive=False):
        table = self.table(u, receive)
        ref, device = table[k][0](), table[k][1]
        src = self.mine(u) if k < 2 and not receive else ref
        return remote(src, ref, self.send.at[(*self.sems(u), k)], self.recv.at[(*self.sems(u), k)], device)

    def keep(self, u):
        return local(self.mine(u), self.table(u, False)[0][0](), self.send.at[(*self.sems(u), self.COPIES)])

    def event(self, k, u):
        ends = self.COPIES - 4
        waits, starts = [], []
        if 0 < 2 * k <= ends:
            waits = [2 * k - 2, 2 * k - 1]
        if 2 * k < ends:
            starts = [2 * k, 2 * k + 1]
        if 2 * k == ends - 4:
            starts += [ends]
        if 2 * k == ends - 2:
            starts += [ends + 1, ends + 2]
        if 2 * k == ends:
            starts = [ends + 3]
        if 2 * k > ends:
            waits = range(ends, ends + 4)
        if k == 0:
            self.keep(u).start()
        for i in waits:
            self.copy(i, u, True).wait_recv()
        if k == 2:
            self.keep(u).wait()
        for i in starts:
            self.copy(i, u).start()

    def drain(self, u):
        for k in range(self.COPIES):
            self.copy(k, u).wait_send()


class GatherUp(Gather):
    COPIES = 12

    def __init__(self, which, *rest):
        super().__init__(*rest)
        self.which = which
        self.axes = "yx" if which else "xy"

    def sems(self, u):
        return (u, self.which)

    def mine(self, u):
        return self.own.at[u, self.which]

    def row(self, u, b, cols, a):
        full = self.full.reshape(L, RING, RING, JOINED, FF)
        return full.at[div(u, NJ), b, a, :, cols] if self.which else full.at[div(u, NJ), a, b, :, cols]

    def table(self, u, receive):
        p = self.p
        a, b = self.axes

        def cols(lo, size, core=p.core):
            return lambda: aligned(mod(u, NJ) * CH + core * HC + lo, size)

        mine = cols(0, HC)
        given = cols(0, HC, p.other) if receive else mine
        parts = (mine, cols(0, LANES), cols(LANES, LANES))
        first = self.ring(a, lambda by, c: self.row(u, p.index(b), c, p.index(a, by)), parts, receive)
        second = self.ring(b, lambda by, part: self.row(u, p.index(b, by), mine(), part), HALVES, receive)
        return first + second + self.hand(lambda by: self.row(u, p.index(b, by), given(), ALL))


class GatherDown(Gather):
    COPIES = 16
    HALF = D // 2
    CUT = 384
    TICKS = ((0, 1, 2, 3, 4, 7, 9, 10), (5, 6, 7, 8, 9, 12, 14, 16))

    def sems(self, v):
        return (v,)

    def cols(self, core):
        return aligned(core * self.HALF, self.HALF)

    def mine(self, v):
        return self.own.at[v, :, self.cols(self.p.core)]

    def table(self, v, receive):
        p = self.p
        x, y, z = (p.index(a) for a in "xyz")
        given = p.other if receive else p.core
        start = p.core * self.HALF
        parts = (lambda: self.cols(p.core), lambda: aligned(start, self.CUT), lambda: aligned(start + self.CUT, self.HALF - self.CUT))
        full = self.full.reshape(L, RING, RING, RING, DROWS, D)
        first = self.ring("x", lambda by, c: full.at[v, p.index("x", by), y, z, :, c], parts, receive)
        second = self.ring("y", lambda by, part: full.at[v, part, p.index("y", by), z, :, self.cols(p.core)], HALVES, receive)
        third = self.ring("z", lambda by, part: full.at[v, part, :, p.index("z", by), :, self.cols(p.core)], HALVES, receive)
        return first + second + third + self.hand(lambda by: full.at[v, :, :, p.index("z", by), :, self.cols(given)])


class Gathers:
    def __init__(self, place, fulls, zcat, wd, us, ur, ds, dr):
        self.ups = [GatherUp(m, place, fulls[m], zcat, us, ur) for m in range(2)]
        self.down = GatherDown(place, fulls[2], wd, ds, dr)

    def tick(self, t):
        for k, (one, two) in enumerate(zip(*GatherDown.TICKS)):

            @pl.when((t == one) | (t == two))
            def _():
                self.down.event(k, jnp.where(t == two, 1, 0))

        for k in range(GATHER_LAG + 1):
            u = t - k

            @pl.when((u >= 0) & (u < UNITS))
            def _():
                for up in self.ups:
                    up.event(k, u)

    def drain(self):
        @pl.loop(0, UNITS)
        def _(u):
            for up in self.ups:
                up.drain(u)

        @pl.loop(0, L)
        def _(v):
            self.down.drain(v)


GATHER_LAG = 5


def along_z(place, wz, zbuf, zcat, send, recv, between):
    z = place.index("z")

    def copy(l, by, receive):
        slot = place.index("z", -by) if receive else z
        return remote(wz.at[l], zbuf.at[slot, l], send.at[l, by - 1], recv.at[l, by - 1], place.to("z", by))

    pairs = [(l, by) for l in range(L) for by in range(1, RING)]
    for l, by in pairs:
        copy(l, by, False).start()
    between()
    zbuf[z] = wz[...]
    for l, by in pairs:
        copy(l, by, True).wait_recv()
    for l, by in pairs:
        copy(l, by, False).wait_send()

    @pl.loop(0, UNITS)
    def _(u):
        for m in range(2):
            pieces = [zbuf[i, div(u, NJ), m, mod(u, NJ)].astype(F32) for i in range(RING)]
            zcat[u, m] = jnp.concatenate(pieces, axis=0).astype(BF)


class Ring:
    def __init__(self, place, axis, src, opposite, block, send, recv):
        self.p, self.axis, self.src, self.opposite, self.block, self.send, self.recv = place, axis, src, opposite, block, send, recv

    def copy(self, k, src, dst):
        return remote(src, dst, self.send(k), self.recv(k), self.p.to(self.axis, -1 if k % 2 else 1))

    def first(self):
        p, a = self.p, self.axis
        far = [self.copy(w, self.src(p.index(a, 2), w), self.opposite(w)) for w in range(2)]
        near = [self.copy(2 + w, self.src(p.index(a, 1 - 2 * w), 1 - w), self.block(w, 1 - w)) for w in range(2)]
        return far + near

    def second(self, sums):
        return [self.copy(4 + w, sums.at[w], self.block(w, w)) for w in range(2)]

    def wait_opposite(self):
        for w in range(2):
            self.copy(w, self.opposite(w), self.opposite(w)).wait_recv()

    def wait_block(self):
        for w in range(2):
            for k, half in ((2, 1 - w), (4, w)):
                self.copy(k + w, self.block(w, half), self.block(w, half)).wait_recv()


def every(lead, body):
    if not lead:
        body(())
        return
    count = 1
    for n in lead:
        count *= n

    @pl.loop(0, count)
    def _(i):
        body((div(i, lead[-1]), mod(i, lead[-1])) if len(lead) == 2 else (i,))


class Reduce:
    EVENTS = 9
    SEMS = 18
    SLOTS = 3
    FAR = 6
    KINDS = {
        "gate": ("xyz", NJ, CH, (RING,), JOINED, ROWS),
        "up": ("yxz", NJ, CH, (RING,), JOINED, ROWS),
        "down": ("zxy", ND, MXU, (RING, RING), DROWS, DROWS),
    }

    def __init__(self, place, kind, term, out, hbm, far, near, sems):
        self.p, self.kind, self.out = place, kind, out
        self.axes, self.n, self.width, self.lead, _, _ = self.KINDS[kind]
        self.down = kind == "down"
        self.term_ref = term.reshape(L, RING, RING, RING, DROWS, D) if self.down else term.reshape(L, RING, RING, JOINED, FF)
        self.half = self.width // 2
        self.count = L * self.n
        self.x1o, self.x1f = hbm
        self.x2o, self.x2f, self.x3o, self.x3f = far
        self.vo, self.vw, self.v1, self.vf, self.s, self.sb, self.v2, self.t, self.tb, self.v3 = near
        self.ls, self.send, self.recv = sems

    @classmethod
    def scratch(cls, kind):
        _, n, w, lead, rows, last = cls.KINDS[kind]
        h, count = w // 2, L * n
        block, mid, end = (*lead, rows), (*lead[1:], rows), (last,)
        dma, vm = pltpu.SemaphoreType.DMA, pltpu.VMEM
        hbm = [jax.ShapeDtypeStruct((count, 2, *block, c), BF) for c in (h, w)]
        far = [vm((cls.FAR, 2, *shape, c), BF) for shape in (mid, end) for c in (h, w)]
        near = [vm((2, *block, h), BF)] * 3 + [vm((3, *block, w), BF)]
        near += [vm((cls.SLOTS, *block, w), F32), vm((cls.SLOTS, *block, w), BF), vm((2, *mid, h), BF)]
        near += [vm((cls.SLOTS, RING, *end, w), F32), vm((cls.SLOTS, RING, *end, w), BF), vm((2, *end, h), BF)]
        return hbm, far, near, [dma((7,)), dma((count, cls.SEMS)), dma((count, cls.SEMS))]

    def halves(self, half):
        return pl.ds(half * self.half, self.half)

    def cut(self, ref, half):
        return ref.at[(ALL,) * (len(ref.shape) - 1) + (self.halves(half),)]

    def layer(self, u):
        return L - 1 - div(u, self.n)

    def term(self, u, q, half=None):
        start = mod(u, self.n) * self.width
        cols = aligned(start, self.width) if half is None else aligned(start + half * self.half, self.half)
        if self.down:
            return self.term_ref.at[self.layer(u), :, :, q, :, cols]
        if self.kind == "up":
            return self.term_ref.at[self.layer(u), :, q, :, cols]
        return self.term_ref.at[self.layer(u), q, :, :, cols]

    def ring(self, phase, u):
        sems = [lambda k, r=r: r.at[u, phase * 6 + k] for r in (self.send, self.recv)]
        far, near = mod(u, self.FAR), mod(u, self.SLOTS)
        if phase == 0:
            src, opposite, block = lambda q, h: self.term(u, q, h), self.x1o.at[u], self.x1f.at[u]
        elif phase == 1:
            src, opposite, block = lambda q, h: self.cut(self.sb.at[near, q], h), self.x2o.at[far], self.x2f.at[far]
        else:
            src, opposite, block = lambda q, h: self.cut(self.tb.at[near, q], h), self.x3o.at[far], self.x3f.at[far]
        return Ring(self.p, self.axes[phase], src, lambda w: opposite.at[w], lambda w, h: self.cut(block.at[w], h), *sems)

    def loads(self, u, blocks):
        a = self.axes[0]
        if blocks:
            pairs = [(self.x1f.at[u, w], self.vf.at[w]) for w in range(2)] + [(self.term(u, self.p.index(a)), self.vf.at[2])]
        else:
            pairs = [(self.x1o.at[u, w], self.vo.at[w]) for w in range(2)]
            pairs += [(self.term(u, self.p.index(a, 1 - 2 * w), w), self.vw.at[w]) for w in range(2)]
        return [local(s, d, self.ls.at[4 * blocks + i]) for i, (s, d) in enumerate(pairs)]

    def wait_sends(self, phase, u, second):
        ring = self.ring(phase, u)
        for copy in ring.second((self.v1, self.v2, self.v3)[phase]) if second else ring.first():
            copy.wait_send()

    def reuse(self, phase, u, second):
        back = 1 if second else self.SLOTS

        @pl.when(u >= back)
        def _():
            self.wait_sends(phase, u - back, second)

    def start(self, u):
        for copy in self.ring(0, u).first():
            copy.start()

    def load_opposite(self, u):
        self.ring(0, u).wait_opposite()
        for copy in self.loads(u, False):
            copy.start()

    def add_opposite(self, u):
        for copy in self.loads(u, False):
            copy.wait()
        self.reuse(0, u, True)

        def add(i):
            for w in range(2):
                self.v1[(w, *i)] = (self.vo[(w, *i)].astype(F32) + self.vw[(w, *i)].astype(F32)).astype(BF)

        every(self.lead, add)
        for copy in self.ring(0, u).second(self.v1):
            copy.start()

    def load_block(self, u):
        self.ring(0, u).wait_block()
        for copy in self.loads(u, True):
            copy.start()

    def add_block(self, u):
        for copy in self.loads(u, True):
            copy.wait()
        self.reuse(1, u, False)
        slot = mod(u, self.SLOTS)

        def add(i):
            own, left, right = (self.vf[(w, *i)].astype(F32) for w in (2, 0, 1))
            total = own + left + right
            self.s[(slot, *i)] = total
            self.sb[(slot, *i)] = total.astype(BF)

        every(self.lead, add)
        for copy in self.ring(1, u).first():
            copy.start()

    def opposite(self, u, phase, lead, kept, came, sums):
        ring = self.ring(phase, u)
        ring.wait_opposite()
        self.reuse(phase, u, True)
        axis = self.axes[phase]
        slot, far = mod(u, self.SLOTS), mod(u, self.FAR)

        def add(i):
            for w in range(2):
                own = kept[(slot, self.p.index(axis, 1 - 2 * w), *i, ALL, self.halves(w))]
                sums[(w, *i)] = (own + came[(far, w, *i)].astype(F32)).astype(BF)

        every(lead, add)
        for copy in ring.second(sums):
            copy.start()

    def middle(self, u):
        self.opposite(u, 1, self.lead[1:], self.s, self.x2o, self.v2)

    def turn(self, u):
        self.ring(1, u).wait_block()
        self.reuse(2, u, False)
        slot, far = mod(u, self.SLOTS), mod(u, self.FAR)
        q = self.p.index(self.axes[1])

        def total(i):
            return self.s[(slot, q, *i)] + self.x2f[(far, 0, *i)].astype(F32) + self.x2f[(far, 1, *i)].astype(F32)

        def put(i, value):
            self.t[slot, i] = value
            self.tb[slot, i] = value.astype(BF)

        if self.down:
            every(self.lead[1:], lambda i: put(*i, total(i)))
        else:
            whole = total(())
            for i in range(RING):
                put(i, whole[ROWS * i : ROWS * (i + 1)])
        for copy in self.ring(2, u).first():
            copy.start()

    def last(self, u):
        self.opposite(u, 2, (), self.t, self.x3o, self.v3)

    def finish(self, u):
        self.ring(2, u).wait_block()
        far = mod(u, self.FAR)
        total = self.t[mod(u, self.SLOTS), self.p.index(self.axes[2])] + self.x3f[far, 0].astype(F32) + self.x3f[far, 1].astype(F32)
        self.out[self.layer(u), :, piece(mod(u, self.n), self.width)] = total.astype(BF)

    def events(self):
        return (self.start, self.load_opposite, self.add_opposite, self.load_block, self.add_block, self.middle, self.turn, self.last, self.finish)

    def drain(self):
        @pl.loop(0, self.count)
        def _(u):
            self.wait_sends(0, u, False)

            @pl.when(u >= self.count - 1)
            def _():
                for phase in range(3):
                    self.wait_sends(phase, u, True)

            @pl.when(u >= self.count - self.SLOTS)
            def _():
                for phase in (1, 2):
                    self.wait_sends(phase, u, False)


class Reduces:
    PERIOD = ND + 2 * NJ + 8
    START = {"down": (2, 3), "gate": (ND + 3, 2), "up": (ND + 3, 2)}
    LAGS = {"down": (0, 3, 4, 7, 8, 10, 12, 14, 16), "gate": (0, 2, 3, 6, 7, 9, 11, 13, 15), "up": (0, 2, 3, 6, 7, 9, 11, 13, 15)}

    def __init__(self, units):
        self.units = units

    def ticks(self):
        return max(first + (u.n - 1) * gap + self.LAGS[u.kind][-1] for u, *_ in self.units for first, gap in (self.START[u.kind],)) + 1

    def tick(self, s):
        order = (0, *range(Reduce.EVENTS - 1, 0, -1))
        for k in order:
            for units in self.units:
                one = units[0]
                first, gap = self.START[one.kind]
                q = s - (first + self.LAGS[one.kind][k])
                r = mod(q, self.PERIOD)

                @pl.when((q >= 0) & (mod(r, gap) == 0) & (r < gap * one.n))
                def _():
                    u = div(q, self.PERIOD) * one.n + div(r, gap)

                    @pl.when(u < one.count)
                    def _():
                        for unit in units:
                            unit.events()[k](u)

    def drain(self):
        for units in self.units:
            for unit in units:
                unit.drain()


def scale_of(wide):
    return lax.rsqrt(jnp.mean(wide * wide, -1, keepdims=True) + 1e-6)


def save_normed(h, rows, a, at, dst, sems, i):
    wide = h.astype(F32)
    tile = (wide * scale_of(wide)).astype(BF)
    a[rows, :] = tile
    slot = mod(i, 2)
    copy = local(at.at[slot], dst.at[:, rows], sems.at[slot])

    @pl.when(i >= 2)
    def _():
        copy.wait()

    at[slot] = tile.T
    copy.start()


def wait_normed(at, dst, sems):
    for slot in range(2):
        local(at.at[slot], dst.at[:, piece(slot, MXU)], sems.at[slot]).wait()


TILE = 4 * MXU


def forward(gathers, fulls, ps, qs, ats, acts, hs, xb, a, at, wb, pq, actt, act, dn, sx, sa, sw, so, sd):
    def weights(l, j):
        return [local(fulls[m].at[l, :, piece(j, CH)], wb.at[mod(j, 2), m], sw.at[mod(j, 2), m]) for m in range(2)]

    def outs(l, s):
        slot = mod(s, 2)
        rows, cols = piece(slot, TILE), piece(div(s, 2), CH)
        pairs = [(pq.at[slot, 0], ps.at[l, rows, cols]), (pq.at[slot, 1], qs.at[l, rows, cols]), (actt.at[slot], acts.at[l, cols, rows])]
        return [local(src, dst, so.at[slot, i]) for i, (src, dst) in enumerate(pairs)]

    keep = local(xb, hs.at[0], sx.at[0])
    keep.start()
    down = local(fulls[2].at[0], dn, sd.at[0])

    @pl.loop(0, GATHER_LAG + 1)
    def _(t):
        gathers.tick(t)

    @pl.loop(0, L)
    def _(l):
        for copy in weights(l, 0):
            copy.start()

        @pl.loop(0, 2 * NJ)
        def _(s):
            j, i = div(s, 2), mod(s, 2)
            slot = mod(j, 2)

            @pl.when(i == 0)
            def _():
                for copy in weights(l, j):
                    copy.wait()

            @pl.when(i == 1)
            def _():
                gathers.tick(GATHER_LAG + 1 + j + l * (NJ + 2))

                @pl.when(j < NJ - 1)
                def _():
                    for copy in weights(l, j + 1):
                        copy.start()

                @pl.when((j == NJ - 1) & (l == 0))
                def _():
                    down.start()

            @pl.when(s >= 2)
            def _():
                for copy in outs(l, s - 2):
                    copy.wait()

            for n in range(TILE // MXU):
                rows = piece(i * (TILE // MXU) + n, MXU)
                part = pl.ds(n * MXU, MXU)
                for half in range(2):
                    cols = pl.ds(half * MXU, MXU)
                    gate, up = (dot(a[rows, :], wb[slot, m, :, cols]) for m in range(2))
                    h = 0.5 * gate
                    t = jnp.tanh(h)
                    e = 1.0 + t
                    silu = h * e
                    pq[i, 0, part, cols] = silu
                    pq[i, 1, part, cols] = (0.5 * up) * (e * (1.0 + h * (1.0 - t)))
                    tile = (silu * up).astype(BF)
                    act[rows, aligned(j * CH + half * MXU, MXU)] = tile
                    actt[i, cols, part] = tile.T
            for copy in outs(l, s):
                copy.start()

        for s in (2 * NJ - 2, 2 * NJ - 1):
            for copy in outs(l, s):
                copy.wait()

        @pl.when(l == 0)
        def _():
            keep.wait()
            down.wait()

            @pl.loop(0, T // CH)
            def _(i):
                @pl.when(mod(i, 2) == 1)
                def _():
                    gathers.tick(GATHER_LAG + NJ + 1 + div(i, 2))

                rows = piece(i, CH)
                y = dot(act[rows, :], dn[...]).astype(BF)
                xb[rows, :] = (xb[rows, :].astype(F32) + y.astype(F32)).astype(BF)
                for n in range(2):
                    sub = piece(2 * i + n, MXU)
                    save_normed(xb[sub, :], sub, a, at, ats.at[1], sa, 2 * i + n)

            wait_normed(at, ats.at[1], sa)
            local(xb, hs.at[1], sx.at[0]).start()

    local(xb, hs.at[1], sx.at[0]).wait()


def by_down(l, base, tick, acts, td, dh, av, st, sl, so):
    load = local(acts.at[l], av, sl)
    load.start()

    def out(i):
        return local(st.at[mod(i, 2)], td.at[l, :, piece(i, MXU)], so.at[mod(i, 2)])

    @pl.loop(0, ND)
    def _(i):
        @pl.when(i == 0)
        def _():
            load.wait()

        @pl.when(i >= 2)
        def _():
            out(i - 2).wait()

        tick(base + i)
        st[mod(i, 2)] = dot(av[...], dh[:, piece(i, MXU)]).astype(BF)
        out(i).start()

    for i in (ND - 2, ND - 1):
        out(i).wait()


def by_gate_and_up(l, base, tick, wdf, ps, qs, ats, dgs, terms, dh, atv, wdb, pq, dgu, stw, sl, sw, sp, sd, so):
    tiles = T // CH

    def weights(j):
        return local(wdf.at[l, piece(j, CH), :], wdb.at[mod(j, 2)], sw.at[mod(j, 2)])

    def factors(s):
        rows, cols, slot = piece(mod(s, tiles), CH), piece(div(s, tiles), CH), mod(s, 2)
        return [local(src.at[l, rows, cols], pq.at[slot, i], sp.at[slot, i]) for i, src in enumerate((ps, qs))]

    def hidden(j):
        return [local(dgu.at[m], dgs[m].at[:, piece(j, CH)], sd.at[m]) for m in range(2)]

    def out(j):
        return [local(stw.at[m], terms[m].at[l, :, piece(j, CH)], so.at[m]) for m in range(2)]

    load = local(ats.at[l], atv, sl)
    weights(0).start()
    for copy in factors(0):
        copy.start()
    load.start()

    def to_hidden(j):
        weights(j).wait()

        @pl.when(j < NJ - 1)
        def _():
            weights(j + 1).start()

        @pl.when(j > 0)
        def _():
            for copy in hidden(j - 1):
                copy.wait()

        @pl.loop(0, tiles)
        def _(i):
            s = j * tiles + i
            slot = mod(s, 2)
            for copy in factors(s):
                copy.wait()

            @pl.when(s < NJ * tiles - 1)
            def _():
                for copy in factors(s + 1):
                    copy.start()

            for n in range(2):
                rows, part = piece(2 * i + n, MXU), pl.ds(n * MXU, MXU)
                by_act = dot(dh[rows, :], wdb[mod(j, 2)], NT).astype(BF).astype(F32)
                for m in range(2):
                    dgu[m, rows, :] = (by_act * pq[slot, 1 - m, part, :]).astype(BF)

        for copy in hidden(j):
            copy.start()

    def to_weights(j):
        @pl.when(j == 0)
        def _():
            load.wait()

        for m in range(2):
            stw[m] = dot(atv[...], dgu[m]).astype(BF)
        for copy in out(j):
            copy.start()

    @pl.loop(0, 2 * NJ)
    def _(h):
        j, late = div(h, 2), mod(h, 2)

        @pl.when((late == 1) & (j > 0))
        def _():
            for copy in out(j - 1):
                copy.wait()

        tick(base + h)
        pl.when(late == 0)(lambda: to_hidden(j))
        pl.when(late == 1)(lambda: to_weights(j))

    for copy in hidden(NJ - 1) + out(NJ - 1):
        copy.wait()


def by_input(l, base, tick, fulls, dgs, hs, dh, wv, gt, ht, sw, sg, sh):
    load = [local(fulls[m].at[l], wv.at[m], sw.at[m]) for m in range(2)]
    tiles = T // MXU

    def rows_of(i):
        rows, slot = piece(i, MXU), mod(i, 2)
        return [local(dgs[m].at[rows, :], gt.at[slot, m], sg.at[slot, m]) for m in range(2)] + [local(hs.at[l, rows, :], ht.at[slot], sh.at[slot])]

    for copy in rows_of(0) + load:
        copy.start()

    @pl.loop(0, tiles)
    def _(i):
        tick(base + i)
        for copy in rows_of(i):
            copy.wait()

        @pl.when(i < tiles - 1)
        def _():
            for copy in rows_of(i + 1):
                copy.start()

        @pl.when(i == 0)
        def _():
            for copy in load:
                copy.wait()

        rows, slot = piece(i, MXU), mod(i, 2)
        by_a = [dot(gt[slot, m], wv[m], NT).astype(BF).astype(F32) for m in range(2)]
        total = by_a[0] + by_a[1]
        wide = ht[slot].astype(F32)
        scale = scale_of(wide)
        along = jnp.mean(total * wide, -1, keepdims=True) * (scale * scale * scale)
        by_h = (total * scale - wide * along).astype(BF).astype(F32)
        dh[rows, :] = (dh[rows, :].astype(F32) + by_h).astype(BF)


def kernel(x, dy, wz, wd, dx, og, ou, od, *refs):
    def take(n):
        nonlocal refs
        head, refs = refs[:n], refs[n:]
        return head

    fulls, (ps, qs, ats, acts, hs), dgs, terms = take(3), take(5), take(2), take(3)
    hbm = [take(2) for _ in KINDS]
    zbuf, zcat, zs, zr = take(4)
    sems = take(4)
    far = [take(4) for _ in KINDS]
    rsems = [take(3) for _ in KINDS]
    sx, sa, sw, so, sd, sp, sg = take(7)
    place = Place()
    place.greet([place.to(a, by) for a in "xy" for by in (1, -1)] + [place.to("z", by) for by in range(1, RING)] + [place.partner()])
    gathers = Gathers(place, fulls, zcat, wd, *sems)
    dma, vm = pltpu.SemaphoreType.DMA, pltpu.VMEM

    def ahead(xb, a, at, wb, pq, actt, act, dn):
        first = local(x, xb, sx.at[0])
        first.start()

        def norm():
            first.wait()

            @pl.loop(0, T // MXU)
            def _(i):
                rows = piece(i, MXU)
                save_normed(xb[rows, :], rows, a, at, ats.at[0], sa, i)

            wait_normed(at, ats.at[0], sa)

        along_z(place, wz, zbuf, zcat, zs, zr, norm)
        forward(gathers, fulls, ps, qs, ats, acts, hs, xb, a, at, wb, pq, actt, act, dn, sx, sa, sw, so, sd)
        gathers.drain()

    pl.run_scoped(
        ahead,
        vm((T, D), BF),
        vm((T, D), BF),
        vm((2, D, MXU), BF),
        vm((2, 2, D, CH), BF),
        vm((2, 2, TILE, CH), F32),
        vm((2, CH, TILE), BF),
        vm((T, FF), BF),
        vm((FF, D), BF),
    )

    def back(dh, *near):
        split = [near[i * 10 : i * 10 + 10] for i in range(3)]
        units = [
            Reduce(place, kind, terms[i], (og, ou, od)[i], hbm[i], far[i], split[i], rsems[i]) for i, kind in enumerate(KINDS)
        ]
        reduces = Reduces([units[2:], units[:2]])
        first = local(dy, dh, sx.at[0])
        first.start()
        first.wait()
        period = Reduces.PERIOD

        @pl.loop(0, L)
        def _(step):
            l, base = L - 1 - step, step * period
            pl.run_scoped(
                lambda av, st: by_down(l, base, reduces.tick, acts, terms[2], dh, av, st, sd.at[0], so.at[0]),
                vm((FF, T), BF),
                vm((2, FF, MXU), BF),
            )
            pl.run_scoped(
                lambda *v: by_gate_and_up(
                    l, base + ND, reduces.tick, fulls[2], ps, qs, ats, dgs, terms, dh, *v, sd.at[0], sw.at[0], sp, sg.at[0], so.at[0]
                ),
                vm((D, T), BF),
                vm((2, CH, D), BF),
                vm((2, 2, CH, CH), F32),
                vm((2, T, CH), BF),
                vm((2, D, CH), BF),
            )
            pl.run_scoped(
                lambda *v: by_input(l, base + ND + 2 * NJ, reduces.tick, fulls, dgs, hs, dh, *v, sw.at[0], sg, sd),
                vm((2, D, FF), BF),
                vm((2, 2, MXU, FF), BF),
                vm((2, MXU, D), BF),
            )

        end = local(dh, dx, sx.at[0])
        end.start()

        @pl.loop(L * period, reduces.ticks() + (L - 1) * period)
        def _(s):
            reduces.tick(s)

        end.wait()
        reduces.drain()

    pl.run_scoped(back, vm((T, D), BF), *(v for kind in KINDS for v in Reduce.scratch(kind)[2]))


KINDS = ("gate", "up", "down")


def call(x, dy, wz, wd):
    made = [Reduce.scratch(kind) for kind in KINDS]
    vmem, hbm = pl.BlockSpec(memory_space=pltpu.VMEM), pl.BlockSpec(memory_space=pltpu.HBM)
    dma, vm = pltpu.SemaphoreType.DMA, pltpu.VMEM

    def shape(*dims, dtype=BF):
        return jax.ShapeDtypeStruct(dims, dtype)

    work = [shape(L, D, FF), shape(L, D, FF), shape(L, FF, D)]
    work += [shape(L, T, FF, dtype=F32), shape(L, T, FF, dtype=F32), shape(L, D, T), shape(L, FF, T), shape(L, T, D)]
    work += [shape(T, FF), shape(T, FF), shape(L, D, FF), shape(L, D, FF), shape(L, FF, D)]
    work += [s for m in made for s in m[0]]
    outs = [shape(L, ROWS, FF), shape(L, ROWS, FF), shape(L, DROWS, D)]
    return pl.pallas_call(
        kernel,
        out_shape=(shape(T, D), *outs, *work),
        in_specs=[hbm, hbm, vmem, vmem],
        out_specs=(hbm, *(vmem for _ in outs), *(hbm for _ in work)),
        scratch_shapes=[
            vm((RING, L, 2, NJ, ROWS, HC), BF),
            vm((UNITS, 2, JOINED, HC), BF),
            dma((L, RING - 1)),
            dma((L, RING - 1)),
            dma((UNITS, 2, GatherUp.COPIES + 1)),
            dma((UNITS, 2, GatherUp.COPIES)),
            dma((L, GatherDown.COPIES + 1)),
            dma((L, GatherDown.COPIES)),
            *(s for m in made for s in m[1]),
            *(s for m in made for s in m[3]),
            dma((1,)),
            dma((2,)),
            dma((2, 2)),
            dma((2, 3)),
            dma((2,)),
            dma((2, 2)),
            dma((2, 2)),
        ],
        name="train",
        compiler_params=pltpu.CompilerParams(collective_id=0, has_side_effects=True, vmem_limit_bytes=67_000_000),
    )(x, dy, wz, wd)[:4]


def solution(mesh):
    def step(x, dy, w_gate, w_up, w_down):
        wz = jnp.stack([w_gate, w_up], 1).reshape(L, 2, ROWS, NJ, 2, HC)
        wz = lax.dynamic_index_in_dim(wz, lax.axis_index("rep"), 4, keepdims=False).transpose(0, 1, 3, 2, 4)
        by_x, *by_w = call(x[0], dy[0], wz, w_down)
        return (by_x[None], *by_w)

    both, rows = P(("rep", "dp"), None, None), P(None, "dp", None)
    return jax.shard_map(
        step,
        mesh=mesh,
        in_specs=(both, both, rows, rows, rows),
        out_specs=(both, *(P("rep", "dp", None),) * 3),
        check_vma=False,
    )
```

time: 2150 us -> 563 us (0.26)
  blocking collectives: 885 us -> 0 us
  Pallas kernels: 0 us -> 548 us
  matrix products: 430 us -> 0 us
  waiting for transfers between devices: 403 us -> 0 us
  starting transfers between devices: 149 us -> 0 us
  local copies, waits for them, and re-layouts: 150 us -> 12 us
  other arithmetic: 102 us -> 0.76 us
    unnamed x2 -> x0, blocking collectives: 885 us -> none
    pallas_call x0 -> x1, Pallas kernels: none -> 548 us  [call(): pl.pallas_call(kernel, out_shape=(shape(T, D), *outs, *work), in_specs=[h...]
    dot_general x17 -> x0, matrix products: 430 us -> none  [the longest x6 158 us: layer(): up = jnp.dot(a, w['w_up'], preferred_element_type=jnp.float32)]
    squeeze x6 -> x0, waiting for transfers between devices: 402 us -> none  [stack(): h = layer(h, {name: w[number] for name, w in weights.items()})]
    unnamed x46 -> x0, starting transfers between devices: 149 us -> none
    unnamed x72 -> x6, local copies, waits for them, and re-layouts: 141 us -> 9.73 us
    unnamed x9 -> x0, other arithmetic: 69.4 us -> none
  transfers between devices with their start and end apart: 52 -> 0, of which waited for: 6 -> 0; matrix products, arithmetic and copies ran while one was open for 64% -> 0% of each run, Pallas kernels for 0% -> 0%
where the time goes in v1:
time: 563 us; the launch traced here: 561 us
  Pallas kernels  548 us (97%)
  local copies, waits for them, and re-layouts  12 us (2%)
    pallas_call x1, Pallas kernels, call(): pl.pallas_call(kernel, out_shape=(shape(T, D), *outs, *work), in_specs=[h...  548 us

profile of v1, /device:TPU:0, one launch (start us, length us, event | category | flops | bytes accessed | tf_op | source)
XLA Modules:
  0.0 561.3 jit_solution(18217969555993897103)
XLA Ops:
  0.6 1.1 stack.9
  1.7 0.1 copy.9
  1.8 1.1 stack.10
  2.9 0.1 copy.10
  3.0 0.8 fusion.1.wz
  3.7 547.8 %train.1 = (bf16[2048,1280]{1,0:T(8,128)(2,1)}, bf16[2,20,3072]{2,1,0:T(8,128)(2,1)}, bf16[2,20,3072]{2,1,0:T(8,128)(2,1)}, bf16[2,48,1280]{2,1,0:T(8,128)(2,1)}...) custom-call(bf16[2048,1280]{1,0:T(8,128)(2,1)} %bitcast.11, ...), custom_call_target="tpu_custom_call" | custom-call | tf_op jit(solution)/shard_map/train/pallas_call | solution.py:908
  551.6 0.0 copy-start
  551.6 1.9 copy.11
  553.5 1.9 copy.12
  555.4 5.2 copy.15
  560.6 0.0 copy-done
  560.6 0.7 copy.16
Async XLA Ops:
  551.6 9.1 %copy-start = (bf16[2,48,1280]{2,1,0:T(8,128)(2,1)S(1)}, bf16[2,48,1280]{2,1,0:T(8,128)(2,1)}, u32[]{:S(2)}) copy-start(bf16[2,48,1280]{2,1,0:T(8,128)(2,1)} %get-tuple-element.23) | copy-start | bytes 737284

commit v2 on v1

--- a/solution.py
+++ b/solution.py
@@ -86,55 +86,56 @@
     def __init__(self, place, full, own, send, recv):
         self.p, self.full, self.own, self.send, self.recv = place, full, own, send, recv
 
-    def ring(self, axis, ref, parts, receive):
-        s, r = (-1, 1) if receive else (0, 0)
+    def ring(self, axis, ref, parts):
         whole, low, high = parts
         right, left = self.p.to(axis, 1), self.p.to(axis, -1)
-        return [(lambda: ref(s, whole()), right), (lambda: ref(r, whole()), left), (lambda: ref(s - 1, low()), right), (lambda: ref(r + 1, high()), left)]
+        return [(lambda: ref(0, whole()), right), (lambda: ref(0, whole()), left), (lambda: ref(-1, low()), right), (lambda: ref(1, high()), left)]
 
     def hand(self, ref):
         return [(lambda by=by: ref(by), self.p.partner()) for by in (0, -1, 1, 2)]
 
-    def copy(self, k, u, receive=False):
-        table = self.table(u, receive)
-        ref, device = table[k][0](), table[k][1]
-        src = self.mine(u) if k < 2 and not receive else ref
-        return remote(src, ref, self.send.at[(*self.sems(u), k)], self.recv.at[(*self.sems(u), k)], device)
+    def copy(self, k, u):
+        ref, device = self.table(u)[k][0](), self.table(u)[k][1]
+        group = min(k // 2, self.GROUPS - 1)
+        return remote(self.mine(u) if k < 2 else ref, ref, self.send.at[(*self.sems(u), group)], self.recv.at[(*self.sems(u), group)], device)
+
+    def all_of(self, group, u):
+        blocks = RING ** (group // 2) * (1 if group % 2 else 2)
+        ref = self.some(u, RING**self.RINGS if group == self.GROUPS - 1 else blocks)
+        return remote(ref, ref, self.send.at[(*self.sems(u), group)], self.recv.at[(*self.sems(u), group)], self.p.partner())
 
     def keep(self, u):
-        return local(self.mine(u), self.table(u, False)[0][0](), self.send.at[(*self.sems(u), self.COPIES)])
+        return local(self.mine(u), self.table(u)[0][0](), self.send.at[(*self.sems(u), self.GROUPS)])
 
     def event(self, k, u):
-        ends = self.COPIES - 4
-        waits, starts = [], []
-        if 0 < 2 * k <= ends:
-            waits = [2 * k - 2, 2 * k - 1]
-        if 2 * k < ends:
-            starts = [2 * k, 2 * k + 1]
-        if 2 * k == ends - 4:
-            starts += [ends]
-        if 2 * k == ends - 2:
-            starts += [ends + 1, ends + 2]
-        if 2 * k == ends:
-            starts = [ends + 3]
-        if 2 * k > ends:
-            waits = range(ends, ends + 4)
+        ends = 2 * self.RINGS
+        starts = [2 * k, 2 * k + 1] if k < ends else []
+        hand = {ends - 2: [0], ends - 1: [1, 2], ends: [3]}.get(k, [])
         if k == 0:
             self.keep(u).start()
-        for i in waits:
-            self.copy(i, u, True).wait_recv()
+        else:
+            self.all_of(k - 1, u).wait_recv()
         if k == 2:
             self.keep(u).wait()
-        for i in starts:
+        for i in starts + [2 * ends + i for i in hand]:
             self.copy(i, u).start()
 
     def drain(self, u):
-        for k in range(self.COPIES):
-            self.copy(k, u).wait_send()
+        for group in range(self.GROUPS):
+            self.all_of(group, u).wait_send()
+
+
+def first_blocks(count, dims):
+    index = []
+    for _ in range(dims):
+        index.insert(0, ALL if count >= RING else pl.ds(0, count) if count > 1 else 0)
+        count = max(count // RING, 1)
+    return tuple(index)
 
 
 class GatherUp(Gather):
-    COPIES = 12
+    RINGS = 2
+    GROUPS = 2 * RINGS + 1
 
     def __init__(self, which, *rest):
         super().__init__(*rest)
@@ -151,50 +152,58 @@
         full = self.full.reshape(L, RING, RING, JOINED, FF)
         return full.at[div(u, NJ), b, a, :, cols] if self.which else full.at[div(u, NJ), a, b, :, cols]
 
-    def table(self, u, receive):
+    def cols(self, u, lo=0, size=HC):
+        return aligned(mod(u, NJ) * CH + self.p.core * HC + lo, size)
+
+    def some(self, u, count):
+        return self.full.reshape(L, RING, RING, JOINED, FF).at[(div(u, NJ), *first_blocks(count, 2), ALL, self.cols(u))]
+
+    def table(self, u):
         p = self.p
         a, b = self.axes
-
-        def cols(lo, size, core=p.core):
-            return lambda: aligned(mod(u, NJ) * CH + core * HC + lo, size)
-
-        mine = cols(0, HC)
-        given = cols(0, HC, p.other) if receive else mine
-        parts = (mine, cols(0, LANES), cols(LANES, LANES))
-        first = self.ring(a, lambda by, c: self.row(u, p.index(b), c, p.index(a, by)), parts, receive)
-        second = self.ring(b, lambda by, part: self.row(u, p.index(b, by), mine(), part), HALVES, receive)
-        return first + second + self.hand(lambda by: self.row(u, p.index(b, by), given(), ALL))
+        parts = (lambda: self.cols(u), lambda: self.cols(u, 0, LANES), lambda: self.cols(u, LANES, LANES))
+        first = self.ring(a, lambda by, c: self.row(u, p.index(b), c, p.index(a, by)), parts)
+        second = self.ring(b, lambda by, part: self.row(u, p.index(b, by), self.cols(u), part), HALVES)
+        return first + second + self.hand(lambda by: self.row(u, p.index(b, by), self.cols(u), ALL))
 
 
 class GatherDown(Gather):
-    COPIES = 16
+    RINGS = 3
+    GROUPS = 2 * RINGS + 1
     HALF = D // 2
     CUT = 384
-    TICKS = ((0, 1, 2, 3, 4, 7, 9, 10), (5, 6, 7, 8, 9, 12, 14, 16))
+    TICKS = ((2, 6, 7, 9, 11, 19, 23, 24), (14, 16, 24, 27, 29, 35, 40, 41))
 
     def sems(self, v):
         return (v,)
 
-    def cols(self, core):
-        return aligned(core * self.HALF, self.HALF)
+    def cols(self):
+        return aligned(self.p.core * self.HALF, self.HALF)
 
     def mine(self, v):
-        return self.own.at[v, :, self.cols(self.p.core)]
-
-    def table(self, v, receive):
+        return self.own.at[v, :, self.cols()]
+
+    def some(self, v, count):
+        return self.full.reshape(L, RING, RING, RING, DROWS, D).at[(v, *first_blocks(count, 3), ALL, self.cols())]
+
+    def table(self, v):
         p = self.p
         x, y, z = (p.index(a) for a in "xyz")
-        given = p.other if receive else p.core
         start = p.core * self.HALF
-        parts = (lambda: self.cols(p.core), lambda: aligned(start, self.CUT), lambda: aligned(start + self.CUT, self.HALF - self.CUT))
+        parts = (self.cols, lambda: aligned(start, self.CUT), lambda: aligned(start + self.CUT, self.HALF - self.CUT))
         full = self.full.reshape(L, RING, RING, RING, DROWS, D)
-        first = self.ring("x", lambda by, c: full.at[v, p.index("x", by), y, z, :, c], parts, receive)
-        second = self.ring("y", lambda by, part: full.at[v, part, p.index("y", by), z, :, self.cols(p.core)], HALVES, receive)
-        third = self.ring("z", lambda by, part: full.at[v, part, :, p.index("z", by), :, self.cols(p.core)], HALVES, receive)
-        return first + second + third + self.hand(lambda by: full.at[v, :, :, p.index("z", by), :, self.cols(given)])
+        first = self.ring("x", lambda by, c: full.at[v, p.index("x", by), y, z, :, c], parts)
+        second = self.ring("y", lambda by, part: full.at[v, part, p.index("y", by), z, :, self.cols()], HALVES)
+        third = self.ring("z", lambda by, part: full.at[v, part, :, p.index("z", by), :, self.cols()], HALVES)
+        return first + second + third + self.hand(lambda by: full.at[v, :, :, p.index("z", by), :, self.cols()])
 
 
 class Gathers:
+    GAP = 2
+    LAGS = (0, 4, 7, 10, 12, 13)
+    AHEAD = LAGS[-1] + 1
+    DEEP = T // CH
+
     def __init__(self, place, fulls, zcat, wd, us, ur, ds, dr):
         self.ups = [GatherUp(m, place, fulls[m], zcat, us, ur) for m in range(2)]
         self.down = GatherDown(place, fulls[2], wd, ds, dr)
@@ -206,10 +215,11 @@
             def _():
                 self.down.event(k, jnp.where(t == two, 1, 0))
 
-        for k in range(GATHER_LAG + 1):
-            u = t - k
-
-            @pl.when((u >= 0) & (u < UNITS))
+        for k in reversed(range(len(self.LAGS))):
+            q = t - self.LAGS[k]
+            u = div(q, self.GAP)
+
+            @pl.when((q >= 0) & (mod(q, self.GAP) == 0) & (u < UNITS))
             def _():
                 for up in self.ups:
                     up.event(k, u)
@@ -225,57 +235,59 @@
             self.down.drain(v)
 
 
-GATHER_LAG = 5
-
-
-def along_z(place, wz, zbuf, zcat, send, recv, between):
-    z = place.index("z")
-
-    def copy(l, by, receive):
-        slot = place.index("z", -by) if receive else z
-        return remote(wz.at[l], zbuf.at[slot, l], send.at[l, by - 1], recv.at[l, by - 1], place.to("z", by))
-
-    pairs = [(l, by) for l in range(L) for by in range(1, RING)]
-    for l, by in pairs:
-        copy(l, by, False).start()
-    between()
-    zbuf[z] = wz[...]
-    for l, by in pairs:
-        copy(l, by, True).wait_recv()
-    for l, by in pairs:
-        copy(l, by, False).wait_send()
-
-    @pl.loop(0, UNITS)
-    def _(u):
+class AlongZ:
+    def __init__(self, place, wz, zbuf, zcat, send, recv):
+        self.p, self.wz, self.zbuf, self.zcat, self.send, self.recv = place, wz, zbuf, zcat, send, recv
+        self.z = place.index("z")
+
+    def copy(self, l, by, receive):
+        slot = self.p.index("z", -by) if receive else self.z
+        return remote(self.wz.at[l], self.zbuf.at[slot, l], self.send.at[l, by - 1], self.recv.at[l, by - 1], self.p.to("z", by))
+
+    def start(self):
+        for l in range(L):
+            for by in range(1, RING):
+                self.copy(l, by, False).start()
+        self.zbuf[self.z] = self.wz[...]
+
+    def wait(self, l):
+        for by in range(1, RING):
+            self.copy(l, by, True).wait_recv()
+        for by in range(1, RING):
+            self.copy(l, by, False).wait_send()
+
+    def join(self, u):
         for m in range(2):
-            pieces = [zbuf[i, div(u, NJ), m, mod(u, NJ)].astype(F32) for i in range(RING)]
-            zcat[u, m] = jnp.concatenate(pieces, axis=0).astype(BF)
+            pieces = [self.zbuf[i, div(u, NJ), m, mod(u, NJ)].astype(F32) for i in range(RING)]
+            self.zcat[u, m] = jnp.concatenate(pieces, axis=0).astype(BF)
 
 
 class Ring:
     def __init__(self, place, axis, src, opposite, block, send, recv):
         self.p, self.axis, self.src, self.opposite, self.block, self.send, self.recv = place, axis, src, opposite, block, send, recv
 
-    def copy(self, k, src, dst):
-        return remote(src, dst, self.send(k), self.recv(k), self.p.to(self.axis, -1 if k % 2 else 1))
+    def copy(self, step, part, way, src, dst):
+        return remote(src, dst, self.send(step), self.recv(2 * part + way), self.p.to(self.axis, 1 - 2 * way))
 
     def first(self):
         p, a = self.p, self.axis
-        far = [self.copy(w, self.src(p.index(a, 2), w), self.opposite(w)) for w in range(2)]
-        near = [self.copy(2 + w, self.src(p.index(a, 1 - 2 * w), 1 - w), self.block(w, 1 - w)) for w in range(2)]
+        far = [self.copy(0, 0, w, self.src(p.index(a, 2), w), self.opposite(w)) for w in range(2)]
+        near = [self.copy(0, 1, w, self.src(p.index(a, 1 - 2 * w), 1 - w), self.block(w, 1 - w)) for w in range(2)]
         return far + near
 
     def second(self, sums):
-        return [self.copy(4 + w, sums.at[w], self.block(w, w)) for w in range(2)]
+        return [self.copy(1, 1, w, sums.at[w], self.block(w, w)) for w in range(2)]
 
     def wait_opposite(self):
         for w in range(2):
-            self.copy(w, self.opposite(w), self.opposite(w)).wait_recv()
+            self.copy(0, 0, w, self.opposite(w), self.opposite(w)).wait_recv()
 
     def wait_block(self):
         for w in range(2):
-            for k, half in ((2, 1 - w), (4, w)):
-                self.copy(k + w, self.block(w, half), self.block(w, half)).wait_recv()
+            self.copy(0, 1, w, self.block(w), self.block(w)).wait_recv()
+
+    def wait_sent(self, step, ref):
+        self.copy(step, 0, 0, ref, ref).wait_send()
 
 
 def every(lead, body):
@@ -293,8 +305,7 @@
 
 class Reduce:
     EVENTS = 9
-    SEMS = 18
-    SLOTS = 3
+    SLOTS = 2
     FAR = 6
     KINDS = {
         "gate": ("xyz", NJ, CH, (RING,), JOINED, ROWS),
@@ -325,7 +336,7 @@
         near = [vm((2, *block, h), BF)] * 3 + [vm((3, *block, w), BF)]
         near += [vm((cls.SLOTS, *block, w), F32), vm((cls.SLOTS, *block, w), BF), vm((2, *mid, h), BF)]
         near += [vm((cls.SLOTS, RING, *end, w), F32), vm((cls.SLOTS, RING, *end, w), BF), vm((2, *end, h), BF)]
-        return hbm, far, near, [dma((7,)), dma((count, cls.SEMS)), dma((count, cls.SEMS))]
+        return hbm, far, near, [dma((7,)), dma((cls.FAR, 3 * 2)), dma((cls.FAR, 3 * 4))]
 
     def halves(self, half):
         return pl.ds(half * self.half, self.half)
@@ -346,15 +357,15 @@
         return self.term_ref.at[self.layer(u), q, :, :, cols]
 
     def ring(self, phase, u):
-        sems = [lambda k, r=r: r.at[u, phase * 6 + k] for r in (self.send, self.recv)]
         far, near = mod(u, self.FAR), mod(u, self.SLOTS)
+        sems = (lambda k: self.send.at[far, 2 * phase + k], lambda k: self.recv.at[far, 4 * phase + k])
         if phase == 0:
             src, opposite, block = lambda q, h: self.term(u, q, h), self.x1o.at[u], self.x1f.at[u]
         elif phase == 1:
             src, opposite, block = lambda q, h: self.cut(self.sb.at[near, q], h), self.x2o.at[far], self.x2f.at[far]
         else:
             src, opposite, block = lambda q, h: self.cut(self.tb.at[near, q], h), self.x3o.at[far], self.x3f.at[far]
-        return Ring(self.p, self.axes[phase], src, lambda w: opposite.at[w], lambda w, h: self.cut(block.at[w], h), *sems)
+        return Ring(self.p, self.axes[phase], src, lambda w: opposite.at[w], lambda w, h=None: block.at[w] if h is None else self.cut(block.at[w], h), *sems)
 
     def loads(self, u, blocks):
         a = self.axes[0]
@@ -366,18 +377,19 @@
         return [local(s, d, self.ls.at[4 * blocks + i]) for i, (s, d) in enumerate(pairs)]
 
     def wait_sends(self, phase, u, second):
-        ring = self.ring(phase, u)
-        for copy in ring.second((self.v1, self.v2, self.v3)[phase]) if second else ring.first():
-            copy.wait_send()
+        far = mod(u, self.FAR)
+        sums, blocks = ((self.v1, self.x1f.at[u]), (self.v2, self.x2f.at[far]), (self.v3, self.x3f.at[far]))[phase]
+        self.ring(phase, u).wait_sent(second, sums if second else blocks)
 
     def reuse(self, phase, u, second):
-        back = 1 if second else self.SLOTS
+        back = 1 if second else self.SLOTS if phase else self.FAR
 
         @pl.when(u >= back)
         def _():
             self.wait_sends(phase, u - back, second)
 
     def start(self, u):
+        self.reuse(0, u, False)
         for copy in self.ring(0, u).first():
             copy.start()
 
@@ -476,7 +488,9 @@
     def drain(self):
         @pl.loop(0, self.count)
         def _(u):
-            self.wait_sends(0, u, False)
+            @pl.when(u >= self.count - self.FAR)
+            def _():
+                self.wait_sends(0, u, False)
 
             @pl.when(u >= self.count - 1)
             def _():
@@ -491,8 +505,8 @@
 
 class Reduces:
     PERIOD = ND + 2 * NJ + 8
-    START = {"down": (2, 3), "gate": (ND + 3, 2), "up": (ND + 3, 2)}
-    LAGS = {"down": (0, 3, 4, 7, 8, 10, 12, 14, 16), "gate": (0, 2, 3, 6, 7, 9, 11, 13, 15), "up": (0, 2, 3, 6, 7, 9, 11, 13, 15)}
+    START = {"down": (7, 2), "gate": (ND + 3, 2)}
+    LAGS = {"down": (0, 3, 5, 8, 10, 12, 14, 17, 18), "gate": (0, 2, 3, 7, 8, 10, 12, 14, 16)}
 
     def __init__(self, units):
         self.units = units
@@ -501,8 +515,7 @@
         return max(first + (u.n - 1) * gap + self.LAGS[u.kind][-1] for u, *_ in self.units for first, gap in (self.START[u.kind],)) + 1
 
     def tick(self, s):
-        order = (0, *range(Reduce.EVENTS - 1, 0, -1))
-        for k in order:
+        for k in reversed(range(Reduce.EVENTS)):
             for units in self.units:
                 one = units[0]
                 first, gap = self.START[one.kind]
@@ -551,7 +564,7 @@
 TILE = 4 * MXU
 
 
-def forward(gathers, fulls, ps, qs, ats, acts, hs, xb, a, at, wb, pq, actt, act, dn, sx, sa, sw, so, sd):
+def forward(first, along_z, gathers, fulls, ps, qs, ats, acts, hs, xb, a, at, wb, pq, actt, act, dn, sx, sa, sw, so, sd):
     def weights(l, j):
         return [local(fulls[m].at[l, :, piece(j, CH)], wb.at[mod(j, 2), m], sw.at[mod(j, 2), m]) for m in range(2)]
 
@@ -562,12 +575,31 @@
         return [local(src, dst, so.at[slot, i]) for i, (src, dst) in enumerate(pairs)]
 
     keep = local(xb, hs.at[0], sx.at[0])
+    down = local(fulls[2].at[0], dn, sd.at[0])
+    along_z.start()
+    along_z.wait(0)
+    pl.loop(0, NJ)(along_z.join)
+    first.wait()
     keep.start()
-    down = local(fulls[2].at[0], dn, sd.at[0])
-
-    @pl.loop(0, GATHER_LAG + 1)
+
+    @pl.loop(0, gathers.AHEAD)
     def _(t):
         gathers.tick(t)
+
+        @pl.when(t == 0)
+        def _():
+            along_z.wait(1)
+
+        @pl.when(t < NJ)
+        def _():
+            along_z.join(NJ + t)
+
+        @pl.when(t < T // MXU)
+        def _():
+            rows = piece(t, MXU)
+            save_normed(xb[rows, :], rows, a, at, ats.at[0], sa, t)
+
+    wait_normed(at, ats.at[0], sa)
 
     @pl.loop(0, L)
     def _(l):
@@ -584,10 +616,10 @@
                 for copy in weights(l, j):
                     copy.wait()
 
+            gathers.tick(gathers.AHEAD + l * (2 * NJ + gathers.DEEP) + s)
+
             @pl.when(i == 1)
             def _():
-                gathers.tick(GATHER_LAG + 1 + j + l * (NJ + 2))
-
                 @pl.when(j < NJ - 1)
                 def _():
                     for copy in weights(l, j + 1):
@@ -631,10 +663,7 @@
 
             @pl.loop(0, T // CH)
             def _(i):
-                @pl.when(mod(i, 2) == 1)
-                def _():
-                    gathers.tick(GATHER_LAG + NJ + 1 + div(i, 2))
-
+                gathers.tick(gathers.AHEAD + 2 * NJ + i)
                 rows = piece(i, CH)
                 y = dot(act[rows, :], dn[...]).astype(BF)
                 xb[rows, :] = (xb[rows, :].astype(F32) + y.astype(F32)).astype(BF)
@@ -648,40 +677,61 @@
     local(xb, hs.at[1], sx.at[0]).wait()
 
 
-def by_down(l, base, tick, acts, td, dh, av, st, sl, so):
-    load = local(acts.at[l], av, sl)
-    load.start()
+def by_down(l, base, tick, first, acts, td, dh, av, st, sl, so):
+    parts = 3
+
+    def load(part):
+        rows = piece(part, FF // parts)
+        return local(acts.at[l, rows, :], av.at[rows, :], sl.at[part])
+
+    for part in range(parts):
+        load(part).start()
 
     def out(i):
         return local(st.at[mod(i, 2)], td.at[l, :, piece(i, MXU)], so.at[mod(i, 2)])
 
     @pl.loop(0, ND)
     def _(i):
+        @pl.when(i >= 2)
+        def _():
+            out(i - 2).wait()
+
+        tick(base + i)
+
         @pl.when(i == 0)
         def _():
-            load.wait()
-
-        @pl.when(i >= 2)
-        def _():
-            out(i - 2).wait()
-
-        tick(base + i)
-        st[mod(i, 2)] = dot(av[...], dh[:, piece(i, MXU)]).astype(BF)
+            first()
+
+            @pl.loop(0, parts)
+            def _(part):
+                load(part).wait()
+                rows = piece(part, FF // parts)
+                st[0, rows, :] = dot(av[rows, :], dh[:, :MXU]).astype(BF)
+
+        @pl.when(i > 0)
+        def _():
+            st[mod(i, 2)] = dot(av[...], dh[:, piece(i, MXU)]).astype(BF)
+
         out(i).start()
 
     for i in (ND - 2, ND - 1):
         out(i).wait()
 
 
-def by_gate_and_up(l, base, tick, wdf, ps, qs, ats, dgs, terms, dh, atv, wdb, pq, dgu, stw, sl, sw, sp, sd, so):
-    tiles = T // CH
+def by_gate_and_up(l, base, tick, ahead, wdf, ps, qs, ats, dgs, terms, dh, atv, wdb, pq, dgu, stw, sl, sw, sp, sd, so):
+    tiles = T // TILE
 
     def weights(j):
         return local(wdf.at[l, piece(j, CH), :], wdb.at[mod(j, 2)], sw.at[mod(j, 2)])
 
-    def factors(s):
-        rows, cols, slot = piece(mod(s, tiles), CH), piece(div(s, tiles), CH), mod(s, 2)
-        return [local(src.at[l, rows, cols], pq.at[slot, i], sp.at[slot, i]) for i, src in enumerate((ps, qs))]
+    def factors(j, i):
+        rows, cols = piece(i, TILE), piece(j, CH)
+        return [local(src.at[l, rows, cols], pq.at[m, rows], sp.at[i, m]) for m, src in enumerate((qs, ps))]
+
+    def load_factors(j):
+        for i in range(tiles):
+            for copy in factors(j, i):
+                copy.start()
 
     def hidden(j):
         return [local(dgu.at[m], dgs[m].at[:, piece(j, CH)], sd.at[m]) for m in range(2)]
@@ -691,8 +741,7 @@
 
     load = local(ats.at[l], atv, sl)
     weights(0).start()
-    for copy in factors(0):
-        copy.start()
+    load_factors(0)
     load.start()
 
     def to_hidden(j):
@@ -709,21 +758,16 @@
 
         @pl.loop(0, tiles)
         def _(i):
-            s = j * tiles + i
-            slot = mod(s, 2)
-            for copy in factors(s):
+            for copy in factors(j, i):
                 copy.wait()
 
-            @pl.when(s < NJ * tiles - 1)
-            def _():
-                for copy in factors(s + 1):
-                    copy.start()
-
-            for n in range(2):
-                rows, part = piece(2 * i + n, MXU), pl.ds(n * MXU, MXU)
-                by_act = dot(dh[rows, :], wdb[mod(j, 2)], NT).astype(BF).astype(F32)
-                for m in range(2):
-                    dgu[m, rows, :] = (by_act * pq[slot, 1 - m, part, :]).astype(BF)
+            for n in range(TILE // MXU):
+                rows = piece(i * (TILE // MXU) + n, MXU)
+                for half in range(2):
+                    cols = pl.ds(half * MXU, MXU)
+                    by_act = dot(dh[rows, :], wdb[mod(j, 2), cols, :], NT).astype(BF).astype(F32)
+                    for m in range(2):
+                        dgu[m, rows, cols] = (by_act * pq[m, rows, cols]).astype(BF)
 
         for copy in hidden(j):
             copy.start()
@@ -732,6 +776,14 @@
         @pl.when(j == 0)
         def _():
             load.wait()
+
+        @pl.when(j < NJ - 1)
+        def _():
+            load_factors(j + 1)
+
+        @pl.when(j == NJ - 1)
+        def _():
+            ahead.start()
 
         for m in range(2):
             stw[m] = dot(atv[...], dgu[m]).astype(BF)
@@ -755,15 +807,15 @@
         copy.wait()
 
 
-def by_input(l, base, tick, fulls, dgs, hs, dh, wv, gt, ht, sw, sg, sh):
-    load = [local(fulls[m].at[l], wv.at[m], sw.at[m]) for m in range(2)]
+def by_input(l, base, tick, ahead, full, dgs, hs, dh, first, second, gt, ht, sw, sg, sh):
+    after = local(full.at[l], second, sw)
     tiles = T // MXU
 
     def rows_of(i):
         rows, slot = piece(i, MXU), mod(i, 2)
         return [local(dgs[m].at[rows, :], gt.at[slot, m], sg.at[slot, m]) for m in range(2)] + [local(hs.at[l, rows, :], ht.at[slot], sh.at[slot])]
 
-    for copy in rows_of(0) + load:
+    for copy in rows_of(0) + [after]:
         copy.start()
 
     @pl.loop(0, tiles)
@@ -779,11 +831,11 @@
 
         @pl.when(i == 0)
         def _():
-            for copy in load:
-                copy.wait()
+            ahead.wait()
+            after.wait()
 
         rows, slot = piece(i, MXU), mod(i, 2)
-        by_a = [dot(gt[slot, m], wv[m], NT).astype(BF).astype(F32) for m in range(2)]
+        by_a = [dot(gt[slot, m], w[...], NT).astype(BF).astype(F32) for m, w in enumerate((first, second))]
         total = by_a[0] + by_a[1]
         wide = ht[slot].astype(F32)
         scale = scale_of(wide)
@@ -806,26 +858,15 @@
     rsems = [take(3) for _ in KINDS]
     sx, sa, sw, so, sd, sp, sg = take(7)
     place = Place()
-    place.greet([place.to(a, by) for a in "xy" for by in (1, -1)] + [place.to("z", by) for by in range(1, RING)] + [place.partner()])
     gathers = Gathers(place, fulls, zcat, wd, *sems)
     dma, vm = pltpu.SemaphoreType.DMA, pltpu.VMEM
 
     def ahead(xb, a, at, wb, pq, actt, act, dn):
         first = local(x, xb, sx.at[0])
         first.start()
-
-        def norm():
-            first.wait()
-
-            @pl.loop(0, T // MXU)
-            def _(i):
-                rows = piece(i, MXU)
-                save_normed(xb[rows, :], rows, a, at, ats.at[0], sa, i)
-
-            wait_normed(at, ats.at[0], sa)
-
-        along_z(place, wz, zbuf, zcat, zs, zr, norm)
-        forward(gathers, fulls, ps, qs, ats, acts, hs, xb, a, at, wb, pq, actt, act, dn, sx, sa, sw, so, sd)
+        place.greet([place.to(a, by) for a in "xy" for by in (1, -1)] + [place.to("z", by) for by in range(1, RING)] + [place.partner()])
+        along_z = AlongZ(place, wz, zbuf, zcat, zs, zr)
+        forward(first, along_z, gathers, fulls, ps, qs, ats, acts, hs, xb, a, at, wb, pq, actt, act, dn, sx, sa, sw, so, sd)
         gathers.drain()
 
     pl.run_scoped(
@@ -848,33 +889,39 @@
         reduces = Reduces([units[2:], units[:2]])
         first = local(dy, dh, sx.at[0])
         first.start()
-        first.wait()
         period = Reduces.PERIOD
 
         @pl.loop(0, L)
         def _(step):
             l, base = L - 1 - step, step * period
             pl.run_scoped(
-                lambda av, st: by_down(l, base, reduces.tick, acts, terms[2], dh, av, st, sd.at[0], so.at[0]),
+                lambda av, st: by_down(
+                    l, base, reduces.tick, lambda: pl.when(step == 0)(first.wait), acts, terms[2], dh, av, st, sp.at[0], so.at[0]
+                ),
                 vm((FF, T), BF),
                 vm((2, FF, MXU), BF),
             )
-            pl.run_scoped(
-                lambda *v: by_gate_and_up(
-                    l, base + ND, reduces.tick, fulls[2], ps, qs, ats, dgs, terms, dh, *v, sd.at[0], sw.at[0], sp, sg.at[0], so.at[0]
-                ),
-                vm((D, T), BF),
-                vm((2, CH, D), BF),
-                vm((2, 2, CH, CH), F32),
-                vm((2, T, CH), BF),
-                vm((2, D, CH), BF),
-            )
-            pl.run_scoped(
-                lambda *v: by_input(l, base + ND + 2 * NJ, reduces.tick, fulls, dgs, hs, dh, *v, sw.at[0], sg, sd),
-                vm((2, D, FF), BF),
-                vm((2, 2, MXU, FF), BF),
-                vm((2, MXU, D), BF),
-            )
+
+            def rest(weight):
+                ahead = local(fulls[0].at[l], weight, sx.at[0])
+                pl.run_scoped(
+                    lambda *v: by_gate_and_up(
+                        l, base + ND, reduces.tick, ahead, fulls[2], ps, qs, ats, dgs, terms, dh, *v, sd.at[0], sw.at[0], sp, sg.at[0], so.at[0]
+                    ),
+                    vm((D, T), BF),
+                    vm((2, CH, D), BF),
+                    vm((2, T, CH), F32),
+                    vm((2, T, CH), BF),
+                    vm((2, D, CH), BF),
+                )
+                pl.run_scoped(
+                    lambda *v: by_input(l, base + ND + 2 * NJ, reduces.tick, ahead, fulls[1], dgs, hs, dh, weight, *v, sa.at[0], sg, sd),
+                    vm((D, FF), BF),
+                    vm((2, 2, MXU, FF), BF),
+                    vm((2, MXU, D), BF),
+                )
+
+            pl.run_scoped(rest, vm((D, FF), BF))
 
         end = local(dh, dx, sx.at[0])
         end.start()
@@ -915,10 +962,10 @@
             vm((UNITS, 2, JOINED, HC), BF),
             dma((L, RING - 1)),
             dma((L, RING - 1)),
-            dma((UNITS, 2, GatherUp.COPIES + 1)),
-            dma((UNITS, 2, GatherUp.COPIES)),
-            dma((L, GatherDown.COPIES + 1)),
-            dma((L, GatherDown.COPIES)),
+            dma((UNITS, 2, GatherUp.GROUPS + 1)),
+            dma((UNITS, 2, GatherUp.GROUPS)),
+            dma((L, GatherDown.GROUPS + 1)),
+            dma((L, GatherDown.GROUPS)),
             *(s for m in made for s in m[1]),
             *(s for m in made for s in m[3]),
             dma((1,)),
@@ -926,7 +973,7 @@
             dma((2, 2)),
             dma((2, 3)),
             dma((2,)),
-            dma((2, 2)),
+            dma((2, 3)),
             dma((2, 2)),
         ],
         name="train",

time: 563 us -> 495 us (0.88)
  Pallas kernels: 548 us -> 481 us
    pallas_call x1, Pallas kernels: 548 us -> 481 us  [call(): pl.pallas_call(kernel, out_shape=(shape(T, D), *outs, *work), in_specs=[h...]
where the time goes in v2:
time: 495 us; the launch traced here: 494 us
  Pallas kernels  481 us (97%)
  local copies, waits for them, and re-layouts  12 us (2%)
    pallas_call x1, Pallas kernels, call(): pl.pallas_call(kernel, out_shape=(shape(T, D), *outs, *work), in_specs=[h...  481 us

profile of v2, /device:TPU:0, one launch (start us, length us, event | category | flops | bytes accessed | tf_op | source)
XLA Modules:
  0.0 494.2 jit_solution(11725282199700602626)
XLA Ops:
  0.6 1.1 stack.9
  1.7 0.1 copy.9
  1.8 1.1 stack.10
  2.9 0.1 copy.10
  3.0 0.8 fusion.1.wz
  3.7 480.7 %train.1 = (bf16[2048,1280]{1,0:T(8,128)(2,1)}, bf16[2,20,3072]{2,1,0:T(8,128)(2,1)}, bf16[2,20,3072]{2,1,0:T(8,128)(2,1)}, bf16[2,48,1280]{2,1,0:T(8,128)(2,1)}...) custom-call(bf16[2048,1280]{1,0:T(8,128)(2,1)} %bitcast.11, ...), custom_call_target="tpu_custom_call" | custom-call | tf_op jit(solution)/shard_map/train/pallas_call | solution.py:955
  484.5 0.0 copy-start
  484.5 1.9 copy.11
  486.4 1.9 copy.12
  488.3 5.2 %copy.15 = bf16[1,2048,1280]{2,1,0:T(8,128)(2,1)} copy(bf16[1,2048,1280]{2,1,0:T(8,128)(2,1)} %bitcast.13) | data formatting | bytes 10485760
  493.5 0.0 copy-done
  493.5 0.7 copy.16
Async XLA Ops:
  484.5 9.1 %copy-start = (bf16[2,48,1280]{2,1,0:T(8,128)(2,1)S(1)}, bf16[2,48,1280]{2,1,0:T(8,128)(2,1)}, u32[]{:S(2)}) copy-start(bf16[2,48,1280]{2,1,0:T(8,128)(2,1)} %get-tuple-element.23) | copy-start | bytes 737284

commit v3 on v2

v3 whole, which is shorter than its diff:
```python
import jax
import jax.numpy as jnp
from jax import lax
from jax.experimental import pallas as pl
from jax.experimental.pallas import tpu as pltpu
from jax.sharding import PartitionSpec as P

MESH = pl.DeviceIdType.MESH
BF = jnp.bfloat16
F32 = jnp.float32
L, D, FF, T = 2, 1280, 3072, 2048
BOTH = range(2)
RING = 4
ROWS = D // 64
JOINED = RING * ROWS
DROWS = FF // 64
CH = 512
HC = CH // 2
NJ = FF // CH
UNITS = L * NJ
MXU = 256
ND = D // MXU
ALL = slice(None)
HALVES = (lambda: ALL, lambda: pl.ds(0, 2), lambda: pl.ds(2, 2))
NN = (((1,), (0,)), ((), ()))
NT = (((1,), (1,)), ((), ()))
LANES = 128


def dot(a, b, dims=NN):
    return lax.dot_general(a, b, dims, preferred_element_type=F32)


def local(src, dst, sem):
    return pltpu.make_async_copy(src, dst, sem)


def remote(src, dst, send, recv, device):
    return pltpu.make_async_remote_copy(src_ref=src, dst_ref=dst, send_sem=send, recv_sem=recv, device_id=device, device_id_type=MESH)


def aligned(start, size):
    return pl.ds(pl.multiple_of(start, LANES), size)


def piece(index, size):
    return aligned(index * size, size)


def mod(a, n):
    return lax.rem(a, n)


def div(a, n):
    return lax.div(a, n)


def side(way):
    return 1 - 2 * way


class Place:
    def __init__(self):
        self.core = lax.axis_index("rep")
        self.dp = lax.axis_index("dp")
        self.other = 1 - self.core
        self.place, self.device = {}, {}
        for stride, axis in ((RING**2, "x"), (RING, "y"), (1, "z")):
            at = mod(div(self.dp, stride), RING)
            for by in range(RING):
                self.place[axis, by] = mod(at + by, RING)
                self.device[axis, by] = (self.core, self.dp + (self.place[axis, by] - at) * stride)

    def to(self, axis, by):
        return self.device[axis, by % RING]

    def index(self, axis, by=0):
        return self.place[axis, by % RING]

    def partner(self):
        return (self.other, self.dp)

    def greet(self, others):
        barrier = pltpu.get_barrier_semaphore()
        for other in others:
            pl.semaphore_signal(barrier, inc=1, device_id=other, device_id_type=MESH)
        pl.semaphore_wait(barrier, len(others))


class Gather:
    def __init__(self, place, full, own, send, recv):
        self.p, self.full, self.own, self.send, self.recv = place, full, own, send, recv

    def ring(self, axis, ref, parts):
        whole, low, high = parts
        right, left = self.p.to(axis, 1), self.p.to(axis, -1)
        return [(lambda: ref(0, whole()), right), (lambda: ref(0, whole()), left), (lambda: ref(-1, low()), right), (lambda: ref(1, high()), left)]

    def hand(self, ref):
        return [(lambda by=by: ref(by), self.p.partner()) for by in (0, -1, 1, 2)]

    def copy(self, k):
        ref, device = self.table()[k][0](), self.table()[k][1]
        group = min(k // 2, self.GROUPS - 1)
        return remote(self.mine() if k < 2 else ref, ref, self.send.at[(*self.slot, group)], self.recv.at[(*self.slot, group)], device)

    def all_of(self, group):
        blocks = RING ** (group // 2) * (1 if group % 2 else 2)
        ref = self.some(RING**self.RINGS if group == self.GROUPS - 1 else blocks)
        return remote(ref, ref, self.send.at[(*self.slot, group)], self.recv.at[(*self.slot, group)], self.p.partner())

    def keep(self):
        return local(self.mine(), self.table()[0][0](), self.send.at[(*self.slot, self.GROUPS)])

    def event(self, k, l, j=0):
        self.unit(l, j)
        ends = 2 * self.RINGS
        starts = [2 * k, 2 * k + 1] if k < ends else []
        hand = {ends - 2: [0], ends - 1: [1, 2], ends: [3]}.get(k, [])
        if k < ends:
            self.free(k)
        if k == ends - 2:
            self.free(ends)
        if k == 0:
            self.keep().start()
        else:
            self.all_of(k - 1).wait_recv()
        if k == 2:
            self.keep().wait()
        for i in starts + [2 * ends + i for i in hand]:
            self.copy(i).start()

    def free(self, group):
        pass

    def drain(self, l, j=0):
        self.unit(l, j)
        for group in range(self.GROUPS):
            self.all_of(group).wait_send()


def first_blocks(count, dims):
    index = []
    for _ in range(dims):
        index.insert(0, ALL if count >= RING else pl.ds(0, count) if count > 1 else 0)
        count = max(count // RING, 1)
    return tuple(index)


class GatherUp(Gather):
    RINGS = 2
    GROUPS = 2 * RINGS + 1

    def __init__(self, which, *rest):
        super().__init__(*rest)
        self.which = which
        self.axes = "yx" if which else "xy"

    def unit(self, l, j):
        self.l, self.j, self.slot = l, j, (j, self.which)
        self.start = j * CH + self.p.core * HC

    def free(self, group):
        @pl.when(self.l > 0)
        def _():
            self.all_of(group).wait_send()

    def mine(self):
        return self.own.at[self.l * NJ + self.j, self.which]

    def cols(self, lo=0, size=HC):
        return aligned(self.start + lo, size)

    def view(self):
        return self.full.reshape(L, RING, RING, JOINED, FF)

    def row(self, b, cols, a):
        return self.view().at[self.l, b, a, :, cols] if self.which else self.view().at[self.l, a, b, :, cols]

    def some(self, count):
        return self.view().at[(self.l, *first_blocks(count, 2), ALL, self.cols())]

    def table(self):
        p = self.p
        a, b = self.axes
        parts = (self.cols, lambda: self.cols(0, LANES), lambda: self.cols(LANES, LANES))
        first = self.ring(a, lambda by, c: self.row(p.index(b), c, p.index(a, by)), parts)
        second = self.ring(b, lambda by, part: self.row(p.index(b, by), self.cols(), part), HALVES)
        return first + second + self.hand(lambda by: self.row(p.index(b, by), self.cols(), ALL))


class GatherDown(Gather):
    RINGS = 3
    GROUPS = 2 * RINGS + 1
    HALF = D // 2
    CUT = 384
    TICKS = ((0, 3, 7, 13, 16, 23, 26, 27), (20, 24, 26, 29, 31, 38, 42, 43))

    def unit(self, l, _):
        self.l, self.slot = l, (l,)

    def cols(self):
        return aligned(self.p.core * self.HALF, self.HALF)

    def mine(self):
        return self.own.at[self.l, :, self.cols()]

    def view(self):
        return self.full.reshape(L, RING, RING, RING, DROWS, D)

    def some(self, count):
        return self.view().at[(self.l, *first_blocks(count, 3), ALL, self.cols())]

    def table(self):
        p = self.p
        x, y, z = (p.index(a) for a in "xyz")
        start = p.core * self.HALF
        parts = (self.cols, lambda: aligned(start, self.CUT), lambda: aligned(start + self.CUT, self.HALF - self.CUT))
        full, v = self.view(), self.l
        first = self.ring("x", lambda by, c: full.at[v, p.index("x", by), y, z, :, c], parts)
        second = self.ring("y", lambda by, part: full.at[v, part, p.index("y", by), z, :, self.cols()], HALVES)
        third = self.ring("z", lambda by, part: full.at[v, part, :, p.index("z", by), :, self.cols()], HALVES)
        return first + second + third + self.hand(lambda by: full.at[v, :, :, p.index("z", by), :, self.cols()])


class Gathers:
    LAGS = (0, 6, 9, 12, 14, 15)
    AHEAD = LAGS[-1] + 1
    DEEP = T // CH

    def __init__(self, place, fulls, zcat, wd, us, ur, ds, dr):
        self.ups = [GatherUp(m, place, fulls[m], zcat, us, ur) for m in BOTH]
        self.down = GatherDown(place, fulls[2], wd, ds, dr)

    def tick(self, t):
        for odd in BOTH:

            @pl.when(t & 1 == odd)
            def _():
                for k in reversed(range(len(self.LAGS))):
                    if self.LAGS[k] % 2 == odd:
                        self.step(k, t - self.LAGS[k])

        for k, (one, two) in enumerate(zip(*GatherDown.TICKS)):

            @pl.when((t == one) | (t == two))
            def _():
                self.down.event(k, jnp.where(t == two, 1, 0))

    def step(self, k, q):
        @pl.when((q >= 0) & (q < 2 * UNITS))
        def _():
            u = q >> 1
            l = jnp.where(u >= NJ, 1, 0)
            for up in self.ups:
                up.event(k, l, u - NJ * l)

    def drain(self):
        @pl.loop(0, NJ)
        def _(j):
            for up in self.ups:
                up.drain(L - 1, j)

        @pl.loop(0, L)
        def _(v):
            self.down.drain(v)


class AlongZ:
    def __init__(self, place, wz, zbuf, zcat, send, recv):
        self.p, self.wz, self.zbuf, self.zcat, self.send, self.recv = place, wz, zbuf, zcat, send, recv
        self.z = place.index("z")

    PARTS = (0, 1, 3, NJ, UNITS)

    def copy(self, part, by, receive):
        units = pl.ds(self.PARTS[part], self.PARTS[part + 1] - self.PARTS[part])
        slot = self.p.index("z", -by) if receive else self.z
        sems = (self.send.at[part, by - 1], self.recv.at[part, by - 1])
        return remote(self.wz.at[units], self.zbuf.at[slot, units], *sems, self.p.to("z", by))

    def start(self):
        for part in range(len(self.PARTS) - 1):
            for by in range(1, RING):
                self.copy(part, by, False).start()
        self.zbuf[self.z] = self.wz[...]

    def finish(self, part):
        for receive in (True, False):
            for by in range(1, RING):
                copy = self.copy(part, by, receive)
                copy.wait_recv() if receive else copy.wait_send()

        @pl.loop(self.PARTS[part], self.PARTS[part + 1])
        def _(u):
            for m in BOTH:
                pieces = [self.zbuf[i, u, m].astype(F32) for i in range(RING)]
                self.zcat[u, m] = jnp.concatenate(pieces, axis=0).astype(BF)


class Ring:
    def __init__(self, place, axis, src, opposite, block, send, recv):
        self.p, self.axis, self.src, self.opposite, self.block, self.send, self.recv = place, axis, src, opposite, block, send, recv

    def copy(self, step, part, way, src, dst):
        return remote(src, dst, self.send(step), self.recv(2 * part + way), self.p.to(self.axis, side(way)))

    def first(self):
        p, a = self.p, self.axis
        far = [self.copy(0, 0, w, self.src(p.index(a, 2), w), self.opposite(w)) for w in BOTH]
        near = [self.copy(0, 1, w, self.src(p.index(a, side(w)), 1 - w), self.block(w, 1 - w)) for w in BOTH]
        return far + near

    def second(self, sums):
        return [self.copy(1, 1, w, sums.at[w], self.block(w, w)) for w in BOTH]

    def wait_opposite(self):
        for w in BOTH:
            self.copy(0, 0, w, self.opposite(w), self.opposite(w)).wait_recv()

    def wait_block(self):
        for w in BOTH:
            self.copy(0, 1, w, self.block(w), self.block(w)).wait_recv()

    def wait_sent(self, step, ref):
        self.copy(step, 0, 0, ref, ref).wait_send()


def every(lead, body):
    if not lead:
        body(())
        return
    count = 1
    for n in lead:
        count *= n

    @pl.loop(0, count)
    def _(i):
        body((div(i, lead[-1]), mod(i, lead[-1])) if len(lead) == 2 else (i,))


class Reduce:
    EVENTS = 9
    SLOTS = 2
    KINDS = {
        "gate": ("xyz", NJ, CH, (RING,), JOINED, ROWS),
        "up": ("yxz", NJ, CH, (RING,), JOINED, ROWS),
        "down": ("zxy", ND, MXU, (RING, RING), DROWS, DROWS),
    }

    def __init__(self, place, kind, term, out, hbm, far, near, sems):
        self.p, self.kind, self.out = place, kind, out
        self.axes, self.n, self.width, self.lead, _, _ = self.KINDS[kind]
        self.down = kind == "down"
        self.term_ref = term.reshape(L, RING, RING, RING, DROWS, D) if self.down else term.reshape(L, RING, RING, JOINED, FF)
        self.half = self.width // 2
        self.count = L * self.n
        self.x1o, self.x1f = hbm
        self.x2o, self.x2f, self.x3o, self.x3f = far
        self.vo, self.vw, self.v1, self.vf, self.s, self.sb, self.v2, self.t, self.tb, self.v3 = near
        self.ls, self.send, self.recv = sems

    def unit(self, step, j):
        self.l, self.j, self.u = L - 1 - step, j, step * self.n + j
        self.slot = self.u & 1

    @classmethod
    def scratch(cls, kind):
        _, n, w, lead, rows, last = cls.KINDS[kind]
        h, count = w // 2, L * n
        block, mid, end = (*lead, rows), (*lead[1:], rows), (last,)
        dma, vm = pltpu.SemaphoreType.DMA, pltpu.VMEM
        hbm = [jax.ShapeDtypeStruct((count, 2, *block, c), BF) for c in (h, w)]
        far = [vm((n, 2, *shape, c), BF) for shape in (mid, end) for c in (h, w)]
        near = [vm((2, *block, h), BF)] * 3 + [vm((3, *block, w), BF)]
        near += [vm((cls.SLOTS, *block, w), F32), vm((cls.SLOTS, *block, w), BF), vm((2, *mid, h), BF)]
        near += [vm((cls.SLOTS, RING, *end, w), F32), vm((cls.SLOTS, RING, *end, w), BF), vm((2, *end, h), BF)]
        return hbm, far, near, [dma((7,)), dma((n, 3 * 2)), dma((n, 3 * 4))]

    def halves(self, half):
        return pl.ds(half * self.half, self.half)

    def cut(self, ref, half):
        return ref.at[(ALL,) * (len(ref.shape) - 1) + (self.halves(half),)]

    def term(self, q, half=None):
        start = self.j * self.width
        cols = aligned(start, self.width) if half is None else aligned(start + half * self.half, self.half)
        if self.down:
            return self.term_ref.at[self.l, :, :, q, :, cols]
        if self.kind == "up":
            return self.term_ref.at[self.l, :, q, :, cols]
        return self.term_ref.at[self.l, q, :, :, cols]

    def ring(self, phase, j=None):
        j = self.j if j is None else j
        sems = (lambda k: self.send.at[j, 2 * phase + k], lambda k: self.recv.at[j, 4 * phase + k])
        if phase == 0:
            src, opposite, block = self.term, self.x1o.at[self.u], self.x1f.at[self.u]
        elif phase == 1:
            src, opposite, block = lambda q, h: self.cut(self.sb.at[self.slot, q], h), self.x2o.at[j], self.x2f.at[j]
        else:
            src, opposite, block = lambda q, h: self.cut(self.tb.at[self.slot, q], h), self.x3o.at[j], self.x3f.at[j]
        return Ring(self.p, self.axes[phase], src, lambda w: opposite.at[w], lambda w, h=None: block.at[w] if h is None else self.cut(block.at[w], h), *sems)

    def loads(self, blocks):
        a = self.axes[0]
        if blocks:
            pairs = [(self.x1f.at[self.u, w], self.vf.at[w]) for w in BOTH] + [(self.term(self.p.index(a)), self.vf.at[2])]
        else:
            pairs = [(self.x1o.at[self.u, w], self.vo.at[w]) for w in BOTH]
            pairs += [(self.term(self.p.index(a, side(w)), w), self.vw.at[w]) for w in BOTH]
        return [local(s, d, self.ls.at[4 * blocks + i]) for i, (s, d) in enumerate(pairs)]

    def wait_sends(self, phase, j, second):
        sums, blocks = ((self.v1, self.x1f.at[0]), (self.v2, self.x2f.at[0]), (self.v3, self.x3f.at[0]))[phase]
        self.ring(phase, j).wait_sent(second, sums if second else blocks)

    def reuse(self, phase, second):
        back = 1 if second else self.SLOTS if phase else self.n

        @pl.when(self.u >= back)
        def _():
            j = self.j - back
            self.wait_sends(phase, jnp.where(j < 0, j + self.n, j), second)

    def start(self):
        self.reuse(0, False)
        for copy in self.ring(0).first():
            copy.start()

    def load_opposite(self):
        self.ring(0).wait_opposite()
        for copy in self.loads(False):
            copy.start()

    def add_opposite(self):
        for copy in self.loads(False):
            copy.wait()
        self.reuse(0, True)

        def add(i):
            for w in BOTH:
                self.v1[(w, *i)] = (self.vo[(w, *i)].astype(F32) + self.vw[(w, *i)].astype(F32)).astype(BF)

        every(self.lead, add)
        for copy in self.ring(0).second(self.v1):
            copy.start()

    def load_block(self):
        self.ring(0).wait_block()
        for copy in self.loads(True):
            copy.start()

    def add_block(self):
        for copy in self.loads(True):
            copy.wait()
        self.reuse(1, False)

        def add(i):
            own, left, right = (self.vf[(w, *i)].astype(F32) for w in (2, 0, 1))
            total = own + left + right
            self.s[(self.slot, *i)] = total
            self.sb[(self.slot, *i)] = total.astype(BF)

        every(self.lead, add)
        for copy in self.ring(1).first():
            copy.start()

    def opposite(self, phase, lead, kept, came, sums):
        ring = self.ring(phase)
        ring.wait_opposite()
        self.reuse(phase, True)
        axis = self.axes[phase]

        def add(i):
            for w in BOTH:
                own = kept[(self.slot, self.p.index(axis, side(w)), *i, ALL, self.halves(w))]
                sums[(w, *i)] = (own + came[(self.j, w, *i)].astype(F32)).astype(BF)

        every(lead, add)
        for copy in ring.second(sums):
            copy.start()

    def middle(self):
        self.opposite(1, self.lead[1:], self.s, self.x2o, self.v2)

    def turn(self):
        self.ring(1).wait_block()
        self.reuse(2, False)
        q = self.p.index(self.axes[1])

        def total(i):
            return self.s[(self.slot, q, *i)] + self.x2f[(self.j, 0, *i)].astype(F32) + self.x2f[(self.j, 1, *i)].astype(F32)

        def put(i, value):
            self.t[self.slot, i] = value
            self.tb[self.slot, i] = value.astype(BF)

        if self.down:
            every(self.lead[1:], lambda i: put(*i, total(i)))
        else:
            whole = total(())
            for i in range(RING):
                put(i, whole[ROWS * i : ROWS * (i + 1)])
        for copy in self.ring(2).first():
            copy.start()

    def last(self):
        self.opposite(2, (), self.t, self.x3o, self.v3)

    def finish(self):
        self.ring(2).wait_block()
        total = self.t[self.slot, self.p.index(self.axes[2])] + self.x3f[self.j, 0].astype(F32) + self.x3f[self.j, 1].astype(F32)
        self.out[self.l, :, piece(self.j, self.width)] = total.astype(BF)

    def events(self):
        return (self.start, self.load_opposite, self.add_opposite, self.load_block, self.add_block, self.middle, self.turn, self.last, self.finish)

    def drain(self):
        @pl.loop(0, self.n)
        def _(j):
            self.unit(L - 1, j)
            self.wait_sends(0, j, False)

            @pl.when(j >= self.n - 1)
            def _():
                for phase in range(3):
                    self.wait_sends(phase, j, True)

            @pl.when(j >= self.n - self.SLOTS)
            def _():
                for phase in (1, 2):
                    self.wait_sends(phase, j, False)


class Reduces:
    PERIOD = ND + 1 + 2 * NJ + 8
    START = {"down": 8, "gate": ND + 1 + 3}
    LAGS = {"down": (0, 3, 5, 8, 10, 12, 14, 17, 18), "gate": (0, 2, 3, 7, 8, 10, 12, 14, 16)}

    def __init__(self, units):
        self.units = units

    def after(self):
        return max(self.at(units[0], -1) + 2 * units[0].n - 2 for units in self.units) + 1 - self.PERIOD

    def at(self, unit, k):
        return self.START[unit.kind] + self.LAGS[unit.kind][k]

    def tick(self, step, i):
        for odd in BOTH:

            @pl.when(i & 1 == odd)
            def _():
                for k in reversed(range(Reduce.EVENTS)):
                    for units in self.units:
                        at = self.at(units[0], k)
                        if at % 2 == odd:
                            self.event(units, k, step, i - at)

    def event(self, units, k, step, q):
        early = q < 0
        q = jnp.where(early, q + self.PERIOD, q)
        step = jnp.where(early, step - 1, step)

        @pl.when((q >= 0) & (q < 2 * units[0].n) & (step >= 0) & (step < L))
        def _():
            for unit in units:
                unit.unit(step, q >> 1)
                unit.events()[k]()

    def drain(self):
        for units in self.units:
            for unit in units:
                unit.drain()


def scale_of(wide):
    return lax.rsqrt(jnp.mean(wide * wide, -1, keepdims=True) + 1e-6)


def save_normed(h, rows, a, at, dst, sems, i):
    wide = h.astype(F32)
    tile = (wide * scale_of(wide)).astype(BF)
    a[rows, :] = tile
    slot = mod(i, 2)
    copy = local(at.at[slot], dst.at[:, rows], sems.at[slot])

    @pl.when(i >= 2)
    def _():
        copy.wait()

    at[slot] = tile.T
    copy.start()


def wait_normed(at, dst, sems):
    for slot in BOTH:
        local(at.at[slot], dst.at[:, piece(slot, MXU)], sems.at[slot]).wait()


TILE = 4 * MXU


def forward(first, along_z, gathers, fulls, ps, qs, ats, acts, hs, xb, a, at, wb, pq, actt, act, dn, sx, sa, sw, so, sd):
    def weights(l, j):
        return [local(fulls[m].at[l, :, piece(j, CH)], wb.at[mod(j, 2), m], sw.at[mod(j, 2), m]) for m in BOTH]

    def outs(l, s):
        slot = mod(s, 2)
        rows, cols = piece(slot, TILE), piece(div(s, 2), CH)
        pairs = [(pq.at[slot, 0], ps.at[l, rows, cols]), (pq.at[slot, 1], qs.at[l, rows, cols]), (actt.at[slot], acts.at[l, cols, rows])]
        return [local(src, dst, so.at[slot, i]) for i, (src, dst) in enumerate(pairs)]

    keep = local(xb, hs.at[0], sx.at[0])
    down = local(fulls[2].at[0], dn, sd.at[0])
    along_z.start()
    along_z.finish(0)
    first.wait()
    keep.start()

    @pl.loop(0, gathers.AHEAD)
    def _(t):
        gathers.tick(t)
        for part in range(1, len(AlongZ.PARTS) - 1):

            @pl.when(t == 2 * AlongZ.PARTS[part] - 1)
            def _():
                along_z.finish(part)

        @pl.when(t < T // MXU)
        def _():
            rows = piece(t, MXU)
            save_normed(xb[rows, :], rows, a, at, ats.at[0], sa, t)

    wait_normed(at, ats.at[0], sa)

    for copy in weights(0, 0):
        copy.start()

    @pl.loop(0, L)
    def _(l):
        @pl.loop(0, 2 * NJ)
        def _(s):
            j, i = div(s, 2), mod(s, 2)
            slot = mod(j, 2)

            @pl.when(i == 0)
            def _():
                for copy in weights(l, j):
                    copy.wait()

            gathers.tick(gathers.AHEAD + l * (2 * NJ + gathers.DEEP) + s)

            @pl.when(i == 1)
            def _():
                @pl.when(j < NJ - 1)
                def _():
                    for copy in weights(l, j + 1):
                        copy.start()

                @pl.when((j == NJ - 1) & (l == 0))
                def _():
                    down.start()
                    for copy in weights(1, 0):
                        copy.start()

            @pl.when(s >= 2)
            def _():
                for copy in outs(l, s - 2):
                    copy.wait()

            for n in range(TILE // MXU):
                rows = piece(i * (TILE // MXU) + n, MXU)
                part = pl.ds(n * MXU, MXU)
                for half in BOTH:
                    cols = pl.ds(half * MXU, MXU)
                    gate, up = (dot(a[rows, :], wb[slot, m, :, cols]) for m in BOTH)
                    h = 0.5 * gate
                    t = jnp.tanh(h)
                    e = 1.0 + t
                    silu = h * e
                    pq[i, 0, part, cols] = silu
                    pq[i, 1, part, cols] = (0.5 * up) * (e * (1.0 + h * (1.0 - t)))
                    tile = (silu * up).astype(BF)
                    act[rows, aligned(j * CH + half * MXU, MXU)] = tile
                    actt[i, cols, part] = tile.T
            for copy in outs(l, s):
                copy.start()

        for s in (2 * NJ - 2, 2 * NJ - 1):
            for copy in outs(l, s):
                copy.wait()

        @pl.when(l == 0)
        def _():
            keep.wait()
            down.wait()

            @pl.loop(0, T // CH)
            def _(i):
                gathers.tick(gathers.AHEAD + 2 * NJ + i)
                rows = piece(i, CH)
                y = dot(act[rows, :], dn[...]).astype(BF)
                xb[rows, :] = (xb[rows, :].astype(F32) + y.astype(F32)).astype(BF)
                for n in BOTH:
                    sub = piece(2 * i + n, MXU)
                    save_normed(xb[sub, :], sub, a, at, ats.at[1], sa, 2 * i + n)

            wait_normed(at, ats.at[1], sa)
            local(xb, hs.at[1], sx.at[0]).start()

    local(xb, hs.at[1], sx.at[0]).wait()


def by_down(l, tick, first, acts, td, dh, av, st, sl, so):
    parts = 3

    def load(part):
        rows = piece(part, FF // parts)
        return local(acts.at[l, rows, :], av.at[rows, :], sl.at[part])

    for part in range(parts):
        load(part).start()

    def out(i):
        return local(st.at[mod(i, 2)], td.at[l, :, piece(i, MXU)], so.at[mod(i, 2)])

    @pl.loop(0, ND + 1)
    def _(n):
        i = n - 1

        @pl.when(i >= 2)
        def _():
            out(i - 2).wait()

        tick(n)

        @pl.when(i == 0)
        def _():
            first()

            @pl.loop(0, parts)
            def _(part):
                load(part).wait()
                rows = piece(part, FF // parts)
                st[0, rows, :] = dot(av[rows, :], dh[:, :MXU]).astype(BF)

        @pl.when(i > 0)
        def _():
            st[mod(i, 2)] = dot(av[...], dh[:, piece(i, MXU)]).astype(BF)

        @pl.when(i >= 0)
        def _():
            out(i).start()

    for i in (ND - 2, ND - 1):
        out(i).wait()


def by_gate_and_up(l, tick, ahead, wdf, ps, qs, ats, dgs, terms, dh, atv, wdb, pq, dgu, stw, sl, sw, sp, sd, so):
    tiles = T // TILE

    def weights(j):
        return local(wdf.at[l, piece(j, CH), :], wdb.at[mod(j, 2)], sw.at[mod(j, 2)])

    def factors(j, i):
        rows, cols = piece(i, TILE), piece(j, CH)
        return [local(src.at[l, rows, cols], pq.at[m, rows], sp.at[i, m]) for m, src in enumerate((qs, ps))]

    def load_factors(j):
        for i in range(tiles):
            for copy in factors(j, i):
                copy.start()

    def hidden(j):
        return [local(dgu.at[m], dgs[m].at[:, piece(j, CH)], sd.at[m]) for m in BOTH]

    def out(j):
        return [local(stw.at[m], terms[m].at[l, :, piece(j, CH)], so.at[m]) for m in BOTH]

    load = local(ats.at[l], atv, sl)
    weights(0).start()
    load_factors(0)
    load.start()

    def to_hidden(j):
        weights(j).wait()

        @pl.when(j < NJ - 1)
        def _():
            weights(j + 1).start()

        @pl.when(j > 0)
        def _():
            for copy in hidden(j - 1):
                copy.wait()

        @pl.loop(0, tiles)
        def _(i):
            for copy in factors(j, i):
                copy.wait()

            for n in range(TILE // MXU):
                rows = piece(i * (TILE // MXU) + n, MXU)
                for half in BOTH:
                    cols = pl.ds(half * MXU, MXU)
                    by_act = dot(dh[rows, :], wdb[mod(j, 2), cols, :], NT).astype(BF).astype(F32)
                    for m in BOTH:
                        dgu[m, rows, cols] = (by_act * pq[m, rows, cols]).astype(BF)

        for copy in hidden(j):
            copy.start()

    def to_weights(j):
        @pl.when(j == 0)
        def _():
            load.wait()

        @pl.when(j < NJ - 1)
        def _():
            load_factors(j + 1)

        @pl.when(j == NJ - 1)
        def _():
            ahead.start()

        for m in BOTH:
            stw[m] = dot(atv[...], dgu[m]).astype(BF)
        for copy in out(j):
            copy.start()

    @pl.loop(0, 2 * NJ)
    def _(h):
        j, late = div(h, 2), mod(h, 2)

        @pl.when((late == 1) & (j > 0))
        def _():
            for copy in out(j - 1):
                copy.wait()

        tick(ND + 1 + h)
        pl.when(late == 0)(lambda: to_hidden(j))
        pl.when(late == 1)(lambda: to_weights(j))

    for copy in hidden(NJ - 1) + out(NJ - 1):
        copy.wait()


def by_input(l, tick, ahead, full, dgs, hs, dh, first, second, gt, ht, sw, sg, sh):
    after = local(full.at[l], second, sw)
    tiles = T // MXU

    def rows_of(i):
        rows, slot = piece(i, MXU), mod(i, 2)
        return [local(dgs[m].at[rows, :], gt.at[slot, m], sg.at[slot, m]) for m in BOTH] + [local(hs.at[l, rows, :], ht.at[slot], sh.at[slot])]

    for copy in rows_of(0) + [after]:
        copy.start()

    @pl.loop(0, tiles)
    def _(i):
        tick(ND + 1 + 2 * NJ + i)
        for copy in rows_of(i):
            copy.wait()

        @pl.when(i < tiles - 1)
        def _():
            for copy in rows_of(i + 1):
                copy.start()

        @pl.when(i == 0)
        def _():
            ahead.wait()
            after.wait()

        rows, slot = piece(i, MXU), mod(i, 2)
        by_a = [dot(gt[slot, m], w[...], NT).astype(BF).astype(F32) for m, w in enumerate((first, second))]
        total = by_a[0] + by_a[1]
        wide = ht[slot].astype(F32)
        scale = scale_of(wide)
        along = jnp.mean(total * wide, -1, keepdims=True) * (scale * scale * scale)
        by_h = (total * scale - wide * along).astype(BF).astype(F32)
        dh[rows, :] = (dh[rows, :].astype(F32) + by_h).astype(BF)


def kernel(x, dy, wz, wd, dx, og, ou, od, *refs):
    def take(n):
        nonlocal refs
        head, refs = refs[:n], refs[n:]
        return head

    fulls, (ps, qs, ats, acts, hs), dgs, terms = take(3), take(5), take(2), take(3)
    hbm = [take(2) for _ in KINDS]
    zbuf, zcat, zs, zr = take(4)
    sems = take(4)
    far = [take(4) for _ in KINDS]
    rsems = [take(3) for _ in KINDS]
    sx, sa, sw, so, sd, sp, sg = take(7)
    place = Place()
    gathers = Gathers(place, fulls, zcat, wd, *sems)
    dma, vm = pltpu.SemaphoreType.DMA, pltpu.VMEM

    def ahead(xb, a, at, wb, pq, actt, act, dn):
        first = local(x, xb, sx.at[0])
        first.start()
        place.greet([place.to(a, by) for a in "xy" for by in (1, -1)] + [place.to("z", by) for by in range(1, RING)] + [place.partner()])
        along_z = AlongZ(place, wz, zbuf, zcat, zs, zr)
        forward(first, along_z, gathers, fulls, ps, qs, ats, acts, hs, xb, a, at, wb, pq, actt, act, dn, sx, sa, sw, so, sd)
        gathers.drain()

    pl.run_scoped(
        ahead,
        vm((T, D), BF),
        vm((T, D), BF),
        vm((2, D, MXU), BF),
        vm((2, 2, D, CH), BF),
        vm((2, 2, TILE, CH), F32),
        vm((2, CH, TILE), BF),
        vm((T, FF), BF),
        vm((FF, D), BF),
    )

    def back(dh, *near):
        split = [near[i * 10 : i * 10 + 10] for i in range(3)]
        units = [
            Reduce(place, kind, terms[i], (og, ou, od)[i], hbm[i], far[i], split[i], rsems[i]) for i, kind in enumerate(KINDS)
        ]
        reduces = Reduces([units[2:], units[:2]])
        first = local(dy, dh, sx.at[0])
        first.start()

        @pl.loop(0, L)
        def _(step):
            l = L - 1 - step

            def tick(i):
                reduces.tick(step, i)

            pl.run_scoped(
                lambda av, st: by_down(
                    l, tick, lambda: pl.when(step == 0)(first.wait), acts, terms[2], dh, av, st, sp.at[0], so.at[0]
                ),
                vm((FF, T), BF),
                vm((2, FF, MXU), BF),
            )

            def rest(weight):
                ahead = local(fulls[0].at[l], weight, sx.at[0])
                pl.run_scoped(
                    lambda *v: by_gate_and_up(
                        l, tick, ahead, fulls[2], ps, qs, ats, dgs, terms, dh, *v, sd.at[0], sw.at[0], sp, sg.at[0], so.at[0]
                    ),
                    vm((D, T), BF),
                    vm((2, CH, D), BF),
                    vm((2, T, CH), F32),
                    vm((2, T, CH), BF),
                    vm((2, D, CH), BF),
                )
                pl.run_scoped(
                    lambda *v: by_input(l, tick, ahead, fulls[1], dgs, hs, dh, weight, *v, sa.at[0], sg, sd),
                    vm((D, FF), BF),
                    vm((2, 2, MXU, FF), BF),
                    vm((2, MXU, D), BF),
                )

            pl.run_scoped(rest, vm((D, FF), BF))

        end = local(dh, dx, sx.at[0])
        end.start()

        @pl.loop(0, reduces.after())
        def _(i):
            reduces.tick(L, i)

        end.wait()
        reduces.drain()

    pl.run_scoped(back, vm((T, D), BF), *(v for kind in KINDS for v in Reduce.scratch(kind)[2]))


KINDS = ("gate", "up", "down")


def call(x, dy, wz, wd):
    made = [Reduce.scratch(kind) for kind in KINDS]
    vmem, hbm = pl.BlockSpec(memory_space=pltpu.VMEM), pl.BlockSpec(memory_space=pltpu.HBM)
    dma, vm = pltpu.SemaphoreType.DMA, pltpu.VMEM

    def shape(*dims, dtype=BF):
        return jax.ShapeDtypeStruct(dims, dtype)

    work = [shape(L, D, FF), shape(L, D, FF), shape(L, FF, D)]
    work += [shape(L, T, FF, dtype=F32), shape(L, T, FF, dtype=F32), shape(L, D, T), shape(L, FF, T), shape(L, T, D)]
    work += [shape(T, FF), shape(T, FF), shape(L, D, FF), shape(L, D, FF), shape(L, FF, D)]
    work += [s for m in made for s in m[0]]
    outs = [shape(L, ROWS, FF), shape(L, ROWS, FF), shape(L, DROWS, D)]
    return pl.pallas_call(
        kernel,
        out_shape=(shape(T, D), *outs, *work),
        in_specs=[hbm, hbm, vmem, vmem],
        out_specs=(hbm, *(vmem for _ in outs), *(hbm for _ in work)),
        scratch_shapes=[
            vm((RING, UNITS, 2, ROWS, HC), BF),
            vm((UNITS, 2, JOINED, HC), BF),
            dma((len(AlongZ.PARTS) - 1, RING - 1)),
            dma((len(AlongZ.PARTS) - 1, RING - 1)),
            dma((NJ, 2, GatherUp.GROUPS + 1)),
            dma((NJ, 2, GatherUp.GROUPS)),
            dma((L, GatherDown.GROUPS + 1)),
            dma((L, GatherDown.GROUPS)),
            *(s for m in made for s in m[1]),
            *(s for m in made for s in m[3]),
            dma((1,)),
            dma((2,)),
            dma((2, 2)),
            dma((2, 3)),
            dma((2,)),
            dma((2, 3)),
            dma((2, 2)),
        ],
        name="train",
        compiler_params=pltpu.CompilerParams(collective_id=0, has_side_effects=True, vmem_limit_bytes=67_000_000),
    )(x, dy, wz, wd)[:4]


def solution(mesh):
    def step(x, dy, w_gate, w_up, w_down):
        wz = jnp.stack([w_gate, w_up], 1).reshape(L, 2, ROWS, NJ, 2, HC)
        wz = lax.dynamic_index_in_dim(wz, lax.axis_index("rep"), 4, keepdims=False).transpose(0, 3, 1, 2, 4).reshape(UNITS, 2, ROWS, HC)
        by_x, *by_w = call(x[0], dy[0], wz, w_down)
        return (by_x[None], *by_w)

    both, rows = P(("rep", "dp"), None, None), P(None, "dp", None)
    return jax.shard_map(
        step,
        mesh=mesh,
        in_specs=(both, both, rows, rows, rows),
        out_specs=(both, *(P("rep", "dp", None),) * 3),
        check_vma=False,
    )
```

time: 495 us -> 475 us (0.960)
  Pallas kernels: 481 us -> 460 us
    pallas_call x1, Pallas kernels: 481 us -> 460 us  [call(): pl.pallas_call(kernel, out_shape=(shape(T, D), *outs, *work), in_specs=[h...]
where the time goes in v3:
time: 475 us; the launch traced here: 474 us
  Pallas kernels  460 us (97%)
  local copies, waits for them, and re-layouts  12.7 us (3%)
    pallas_call x1, Pallas kernels, call(): pl.pallas_call(kernel, out_shape=(shape(T, D), *outs, *work), in_specs=[h...  460 us
    unnamed x6, local copies, waits for them, and re-layouts  9.73 us

profile of v3, /device:TPU:0, one launch (start us, length us, event | category | flops | bytes accessed | tf_op | source)
XLA Modules:
  0.0 473.9 jit_solution(12663104469753018055)
XLA Ops:
  0.6 1.1 stack.9
  1.7 1.1 stack.10
  2.8 0.6 dynamic-slice_maximum_fusion
  3.5 0.8 copy.9
  4.3 459.9 %train.1 = (bf16[2048,1280]{1,0:T(8,128)(2,1)}, bf16[2,20,3072]{2,1,0:T(8,128)(2,1)}, bf16[2,20,3072]{2,1,0:T(8,128)(2,1)}, bf16[2,48,1280]{2,1,0:T(8,128)(2,1)}...) custom-call(bf16[2048,1280]{1,0:T(8,128)(2,1)} %bitcast.12, ...), custom_call_target="tpu_custom_call" | custom-call | tf_op jit(solution)/shard_map/train/pallas_call | solution.py:999
  464.2 0.0 copy-start
  464.2 1.9 copy.10
  466.1 1.9 copy.11
  468.0 5.2 %copy.14 = bf16[1,2048,1280]{2,1,0:T(8,128)(2,1)} copy(bf16[1,2048,1280]{2,1,0:T(8,128)(2,1)} %bitcast.14) | data formatting | bytes 10485760
  473.2 0.0 copy-done
  473.2 0.7 copy.15
Async XLA Ops:
  464.2 9.1 %copy-start = (bf16[2,48,1280]{2,1,0:T(8,128)(2,1)S(1)}, bf16[2,48,1280]{2,1,0:T(8,128)(2,1)}, u32[]{:S(2)}) copy-start(bf16[2,48,1280]{2,1,0:T(8,128)(2,1)} %get-tuple-element.23) | copy-start | bytes 737284

commit v4 on v3

--- a/solution.py
+++ b/solution.py
@@ -194,7 +194,7 @@
     GROUPS = 2 * RINGS + 1
     HALF = D // 2
     CUT = 384
-    TICKS = ((0, 3, 7, 13, 16, 23, 26, 27), (20, 24, 26, 29, 31, 38, 42, 43))
+    TICKS = ((-1, 1, 4, 8, 10, 17, 20, 21), (17, 19, 21, 23, 25, 32, 36, 37))
 
     def unit(self, l, _):
         self.l, self.slot = l, (l,)
@@ -224,7 +224,7 @@
 
 
 class Gathers:
-    LAGS = (0, 6, 9, 12, 14, 15)
+    LAGS = (0, 3, 5, 7, 8, 9)
     AHEAD = LAGS[-1] + 1
     DEEP = T // CH
 
@@ -248,12 +248,14 @@
                 self.down.event(k, jnp.where(t == two, 1, 0))
 
     def step(self, k, q):
+        late = q >= 2 * NJ + self.DEEP
+        q = jnp.where(late, q - self.DEEP, jnp.where(q < 2 * NJ, q, -1))
+
         @pl.when((q >= 0) & (q < 2 * UNITS))
         def _():
-            u = q >> 1
-            l = jnp.where(u >= NJ, 1, 0)
+            l = jnp.where(late, 1, 0)
             for up in self.ups:
-                up.event(k, l, u - NJ * l)
+                up.event(k, l, (q >> 1) - NJ * l)
 
     def drain(self):
         @pl.loop(0, NJ)
@@ -324,6 +326,19 @@
 
     def wait_sent(self, step, ref):
         self.copy(step, 0, 0, ref, ref).wait_send()
+
+
+class Spread:
+    def __init__(self, place, axis, src, came, send, recv):
+        self.p, self.axis, self.src, self.came, self.send, self.recv = place, axis, src, came, send, recv
+
+    def start(self):
+        for by in range(1, RING):
+            to = self.p.to(self.axis, by)
+            remote(self.src.at[self.p.index(self.axis, by)], self.came.at[by - 1], self.send, self.recv, to).start()
+
+    def all(self):
+        return remote(self.came, self.came, self.send, self.recv, self.p.to(self.axis, 1))
 
 
 def every(lead, body):
@@ -340,7 +355,7 @@
 
 
 class Reduce:
-    EVENTS = 9
+    EVENTS = 7
     SLOTS = 2
     KINDS = {
         "gate": ("xyz", NJ, CH, (RING,), JOINED, ROWS),
@@ -356,8 +371,8 @@
         self.half = self.width // 2
         self.count = L * self.n
         self.x1o, self.x1f = hbm
-        self.x2o, self.x2f, self.x3o, self.x3f = far
-        self.vo, self.vw, self.v1, self.vf, self.s, self.sb, self.v2, self.t, self.tb, self.v3 = near
+        self.x2, self.x3 = far
+        self.vo, self.vw, self.v1, self.vf, self.s, self.sb, self.t, self.tb = near
         self.ls, self.send, self.recv = sems
 
     def unit(self, step, j):
@@ -371,11 +386,11 @@
         block, mid, end = (*lead, rows), (*lead[1:], rows), (last,)
         dma, vm = pltpu.SemaphoreType.DMA, pltpu.VMEM
         hbm = [jax.ShapeDtypeStruct((count, 2, *block, c), BF) for c in (h, w)]
-        far = [vm((n, 2, *shape, c), BF) for shape in (mid, end) for c in (h, w)]
-        near = [vm((2, *block, h), BF)] * 3 + [vm((3, *block, w), BF)]
-        near += [vm((cls.SLOTS, *block, w), F32), vm((cls.SLOTS, *block, w), BF), vm((2, *mid, h), BF)]
-        near += [vm((cls.SLOTS, RING, *end, w), F32), vm((cls.SLOTS, RING, *end, w), BF), vm((2, *end, h), BF)]
-        return hbm, far, near, [dma((7,)), dma((n, 3 * 2)), dma((n, 3 * 4))]
+        far = [vm((n, RING - 1, *shape, w), BF) for shape in (mid, end)]
+        near = [vm((2, *block, h), BF)] * 2 + [vm((cls.SLOTS, 2, *block, h), BF), vm((3, *block, w), BF)]
+        near += [vm((cls.SLOTS, *block, w), dtype) for dtype in (F32, BF)]
+        near += [vm((cls.SLOTS, RING, *end, w), dtype) for dtype in (F32, BF)]
+        return hbm, far, near, [dma((7,)), dma((n, RING)), dma((n, 2 * RING))]
 
     def halves(self, half):
         return pl.ds(half * self.half, self.half)
@@ -392,16 +407,16 @@
             return self.term_ref.at[self.l, :, q, :, cols]
         return self.term_ref.at[self.l, q, :, :, cols]
 
-    def ring(self, phase, j=None):
+    def ring(self, j=None):
         j = self.j if j is None else j
-        sems = (lambda k: self.send.at[j, 2 * phase + k], lambda k: self.recv.at[j, 4 * phase + k])
-        if phase == 0:
-            src, opposite, block = self.term, self.x1o.at[self.u], self.x1f.at[self.u]
-        elif phase == 1:
-            src, opposite, block = lambda q, h: self.cut(self.sb.at[self.slot, q], h), self.x2o.at[j], self.x2f.at[j]
-        else:
-            src, opposite, block = lambda q, h: self.cut(self.tb.at[self.slot, q], h), self.x3o.at[j], self.x3f.at[j]
-        return Ring(self.p, self.axes[phase], src, lambda w: opposite.at[w], lambda w, h=None: block.at[w] if h is None else self.cut(block.at[w], h), *sems)
+        opposite, block = self.x1o.at[self.u], self.x1f.at[self.u]
+        sems = (lambda k: self.send.at[j, k], lambda k: self.recv.at[j, k])
+        return Ring(self.p, self.axes[0], self.term, lambda w: opposite.at[w], lambda w, h=None: block.at[w] if h is None else self.cut(block.at[w], h), *sems)
+
+    def spread(self, phase, j=None):
+        j = self.j if j is None else j
+        src, came = ((self.sb, self.x2), (self.tb, self.x3))[phase - 1]
+        return Spread(self.p, self.axes[phase], src.at[self.slot], came.at[j], self.send.at[j, 1 + phase], self.recv.at[j, RING - 1 + phase])
 
     def loads(self, blocks):
         a = self.axes[0]
@@ -413,11 +428,13 @@
         return [local(s, d, self.ls.at[4 * blocks + i]) for i, (s, d) in enumerate(pairs)]
 
     def wait_sends(self, phase, j, second):
-        sums, blocks = ((self.v1, self.x1f.at[0]), (self.v2, self.x2f.at[0]), (self.v3, self.x3f.at[0]))[phase]
-        self.ring(phase, j).wait_sent(second, sums if second else blocks)
-
-    def reuse(self, phase, second):
-        back = 1 if second else self.SLOTS if phase else self.n
+        if phase:
+            self.spread(phase, j).all().wait_send()
+        else:
+            self.ring(j).wait_sent(int(second), self.v1.at[0] if second else self.x1f.at[0])
+
+    def reuse(self, phase, second=False):
+        back = self.SLOTS if second or phase else self.n
 
         @pl.when(self.u >= back)
         def _():
@@ -425,12 +442,12 @@
             self.wait_sends(phase, jnp.where(j < 0, j + self.n, j), second)
 
     def start(self):
-        self.reuse(0, False)
-        for copy in self.ring(0).first():
+        self.reuse(0)
+        for copy in self.ring().first():
             copy.start()
 
     def load_opposite(self):
-        self.ring(0).wait_opposite()
+        self.ring().wait_opposite()
         for copy in self.loads(False):
             copy.start()
 
@@ -441,21 +458,21 @@
 
         def add(i):
             for w in BOTH:
-                self.v1[(w, *i)] = (self.vo[(w, *i)].astype(F32) + self.vw[(w, *i)].astype(F32)).astype(BF)
+                self.v1[(self.slot, w, *i)] = (self.vo[(w, *i)].astype(F32) + self.vw[(w, *i)].astype(F32)).astype(BF)
 
         every(self.lead, add)
-        for copy in self.ring(0).second(self.v1):
+        for copy in self.ring().second(self.v1.at[self.slot]):
             copy.start()
 
     def load_block(self):
-        self.ring(0).wait_block()
+        self.ring().wait_block()
         for copy in self.loads(True):
             copy.start()
 
     def add_block(self):
         for copy in self.loads(True):
             copy.wait()
-        self.reuse(1, False)
+        self.reuse(1)
 
         def add(i):
             own, left, right = (self.vf[(w, *i)].astype(F32) for w in (2, 0, 1))
@@ -464,34 +481,20 @@
             self.sb[(self.slot, *i)] = total.astype(BF)
 
         every(self.lead, add)
-        for copy in self.ring(1).first():
-            copy.start()
-
-    def opposite(self, phase, lead, kept, came, sums):
-        ring = self.ring(phase)
-        ring.wait_opposite()
-        self.reuse(phase, True)
-        axis = self.axes[phase]
-
-        def add(i):
-            for w in BOTH:
-                own = kept[(self.slot, self.p.index(axis, side(w)), *i, ALL, self.halves(w))]
-                sums[(w, *i)] = (own + came[(self.j, w, *i)].astype(F32)).astype(BF)
-
-        every(lead, add)
-        for copy in ring.second(sums):
-            copy.start()
-
-    def middle(self):
-        self.opposite(1, self.lead[1:], self.s, self.x2o, self.v2)
+        self.spread(1).start()
+
+    def total(self, own, came):
+        for w in range(RING - 1):
+            own = own + came(w).astype(F32)
+        return own
 
     def turn(self):
-        self.ring(1).wait_block()
-        self.reuse(2, False)
+        self.spread(1).all().wait_recv()
+        self.reuse(2)
         q = self.p.index(self.axes[1])
 
         def total(i):
-            return self.s[(self.slot, q, *i)] + self.x2f[(self.j, 0, *i)].astype(F32) + self.x2f[(self.j, 1, *i)].astype(F32)
+            return self.total(self.s[(self.slot, q, *i)], lambda w: self.x2[(self.j, w, *i)])
 
         def put(i, value):
             self.t[self.slot, i] = value
@@ -503,19 +506,15 @@
             whole = total(())
             for i in range(RING):
                 put(i, whole[ROWS * i : ROWS * (i + 1)])
-        for copy in self.ring(2).first():
-            copy.start()
-
-    def last(self):
-        self.opposite(2, (), self.t, self.x3o, self.v3)
+        self.spread(2).start()
 
     def finish(self):
-        self.ring(2).wait_block()
-        total = self.t[self.slot, self.p.index(self.axes[2])] + self.x3f[self.j, 0].astype(F32) + self.x3f[self.j, 1].astype(F32)
+        self.spread(2).all().wait_recv()
+        total = self.total(self.t[self.slot, self.p.index(self.axes[2])], lambda w: self.x3[self.j, w])
         self.out[self.l, :, piece(self.j, self.width)] = total.astype(BF)
 
     def events(self):
-        return (self.start, self.load_opposite, self.add_opposite, self.load_block, self.add_block, self.middle, self.turn, self.last, self.finish)
+        return (self.start, self.load_opposite, self.add_opposite, self.load_block, self.add_block, self.turn, self.finish)
 
     def drain(self):
         @pl.loop(0, self.n)
@@ -523,21 +522,16 @@
             self.unit(L - 1, j)
             self.wait_sends(0, j, False)
 
-            @pl.when(j >= self.n - 1)
+            @pl.when(j >= self.n - self.SLOTS)
             def _():
                 for phase in range(3):
                     self.wait_sends(phase, j, True)
 
-            @pl.when(j >= self.n - self.SLOTS)
-            def _():
-                for phase in (1, 2):
-                    self.wait_sends(phase, j, False)
-
 
 class Reduces:
     PERIOD = ND + 1 + 2 * NJ + 8
     START = {"down": 8, "gate": ND + 1 + 3}
-    LAGS = {"down": (0, 3, 5, 8, 10, 12, 14, 17, 18), "gate": (0, 2, 3, 7, 8, 10, 12, 14, 16)}
+    LAGS = {"down": (0, 3, 4, 7, 8, 12, 14), "gate": (0, 2, 3, 6, 7, 11, 13)}
 
     def __init__(self, units):
         self.units = units
@@ -616,6 +610,7 @@
     keep = local(xb, hs.at[0], sx.at[0])
     down = local(fulls[2].at[0], dn, sd.at[0])
     along_z.start()
+    gathers.down.event(0, 0)
     along_z.finish(0)
     first.wait()
     keep.start()
@@ -625,7 +620,7 @@
         gathers.tick(t)
         for part in range(1, len(AlongZ.PARTS) - 1):
 
-            @pl.when(t == 2 * AlongZ.PARTS[part] - 1)
+            @pl.when(t == min(2 * AlongZ.PARTS[part], gathers.AHEAD) - 1)
             def _():
                 along_z.finish(part)
 
@@ -663,8 +658,6 @@
                 @pl.when((j == NJ - 1) & (l == 0))
                 def _():
                     down.start()
-                    for copy in weights(1, 0):
-                        copy.start()
 
             @pl.when(s >= 2)
             def _():
@@ -701,6 +694,12 @@
             @pl.loop(0, T // CH)
             def _(i):
                 gathers.tick(gathers.AHEAD + 2 * NJ + i)
+
+                @pl.when(i == T // CH - 1)
+                def _():
+                    for copy in weights(1, 0):
+                        copy.start()
+
                 rows = piece(i, CH)
                 y = dot(act[rows, :], dn[...]).astype(BF)
                 xb[rows, :] = (xb[rows, :].astype(F32) + y.astype(F32)).astype(BF)
@@ -895,7 +894,7 @@
     hbm = [take(2) for _ in KINDS]
     zbuf, zcat, zs, zr = take(4)
     sems = take(4)
-    far = [take(4) for _ in KINDS]
+    far = [take(2) for _ in KINDS]
     rsems = [take(3) for _ in KINDS]
     sx, sa, sw, so, sd, sp, sg = take(7)
     place = Place()
@@ -905,7 +904,7 @@
     def ahead(xb, a, at, wb, pq, actt, act, dn):
         first = local(x, xb, sx.at[0])
         first.start()
-        place.greet([place.to(a, by) for a in "xy" for by in (1, -1)] + [place.to("z", by) for by in range(1, RING)] + [place.partner()])
+        place.greet([place.to(a, by) for a in "xyz" for by in range(1, RING)] + [place.partner()])
         along_z = AlongZ(place, wz, zbuf, zcat, zs, zr)
         forward(first, along_z, gathers, fulls, ps, qs, ats, acts, hs, xb, a, at, wb, pq, actt, act, dn, sx, sa, sw, so, sd)
         gathers.drain()
@@ -923,7 +922,7 @@
     )
 
     def back(dh, *near):
-        split = [near[i * 10 : i * 10 + 10] for i in range(3)]
+        split = [near[i * 8 : i * 8 + 8] for i in range(3)]
         units = [
             Reduce(place, kind, terms[i], (og, ou, od)[i], hbm[i], far[i], split[i], rsems[i]) for i, kind in enumerate(KINDS)
         ]

time: 475 us -> 480 us (1.011)
  Pallas kernels: 460 us -> 465 us
    pallas_call x1, Pallas kernels: 460 us -> 465 us  [call(): pl.pallas_call(kernel, out_shape=(shape(T, D), *outs, *work), in_specs=[h...]
where the time goes in v4:
time: 480 us; the launch traced here: 479 us
  Pallas kernels  465 us (97%)
  local copies, waits for them, and re-layouts  12.7 us (3%)
    pallas_call x1, Pallas kernels, call(): pl.pallas_call(kernel, out_shape=(shape(T, D), *outs, *work), in_specs=[h...  465 us
    unnamed x6, local copies, waits for them, and re-layouts  9.73 us

profile of v4, /device:TPU:0, one launch (start us, length us, event | category | flops | bytes accessed | tf_op | source)
XLA Modules:
  0.0 479.1 jit_solution(8411720346747752228)
XLA Ops:
  0.6 1.1 stack.9
  1.7 1.1 stack.10
  2.8 0.6 dynamic-slice_maximum_fusion
  3.5 0.8 copy.9
  4.3 465.0 %train.1 = (bf16[2048,1280]{1,0:T(8,128)(2,1)}, bf16[2,20,3072]{2,1,0:T(8,128)(2,1)}, bf16[2,20,3072]{2,1,0:T(8,128)(2,1)}, bf16[2,48,1280]{2,1,0:T(8,128)(2,1)}...) custom-call(bf16[2048,1280]{1,0:T(8,128)(2,1)} %bitcast.12, ...), custom_call_target="tpu_custom_call" | custom-call | tf_op jit(solution)/shard_map/train/pallas_call | solution.py:998
  469.3 0.0 copy-start
  469.3 1.9 copy.10
  471.3 1.9 copy.11
  473.2 5.2 %copy.14 = bf16[1,2048,1280]{2,1,0:T(8,128)(2,1)} copy(bf16[1,2048,1280]{2,1,0:T(8,128)(2,1)} %bitcast.14) | data formatting | bytes 10485760
  478.4 0.0 copy-done
  478.4 0.7 copy.15
Async XLA Ops:
  469.3 9.1 %copy-start = (bf16[2,48,1280]{2,1,0:T(8,128)(2,1)S(1)}, bf16[2,48,1280]{2,1,0:T(8,128)(2,1)}, u32[]{:S(2)}) copy-start(bf16[2,48,1280]{2,1,0:T(8,128)(2,1)} %get-tuple-element.23) | copy-start | bytes 737284

commit v5 on v4

--- a/solution.py
+++ b/solution.py
@@ -359,7 +359,7 @@
     SLOTS = 2
     KINDS = {
         "gate": ("xyz", NJ, CH, (RING,), JOINED, ROWS),
-        "up": ("yxz", NJ, CH, (RING,), JOINED, ROWS),
+        "up": ("yzx", NJ, CH, (RING,), JOINED, ROWS),
         "down": ("zxy", ND, MXU, (RING, RING), DROWS, DROWS),
     }
 
@@ -383,12 +383,14 @@
     def scratch(cls, kind):
         _, n, w, lead, rows, last = cls.KINDS[kind]
         h, count = w // 2, L * n
-        block, mid, end = (*lead, rows), (*lead[1:], rows), (last,)
+        block, end = (*lead, rows), (last,)
+        kept = (RING, RING, ROWS) if kind == "up" else block
+        mid = kept[1:]
         dma, vm = pltpu.SemaphoreType.DMA, pltpu.VMEM
         hbm = [jax.ShapeDtypeStruct((count, 2, *block, c), BF) for c in (h, w)]
         far = [vm((n, RING - 1, *shape, w), BF) for shape in (mid, end)]
         near = [vm((2, *block, h), BF)] * 2 + [vm((cls.SLOTS, 2, *block, h), BF), vm((3, *block, w), BF)]
-        near += [vm((cls.SLOTS, *block, w), dtype) for dtype in (F32, BF)]
+        near += [vm((cls.SLOTS, *kept, w), dtype) for dtype in (F32, BF)]
         near += [vm((cls.SLOTS, RING, *end, w), dtype) for dtype in (F32, BF)]
         return hbm, far, near, [dma((7,)), dma((n, RING)), dma((n, 2 * RING))]
 
@@ -477,8 +479,12 @@
         def add(i):
             own, left, right = (self.vf[(w, *i)].astype(F32) for w in (2, 0, 1))
             total = own + left + right
-            self.s[(self.slot, *i)] = total
-            self.sb[(self.slot, *i)] = total.astype(BF)
+            parts = [(i, total)]
+            if self.kind == "up":
+                parts = [((z, *i), total[ROWS * z : ROWS * (z + 1)]) for z in range(RING)]
+            for at, part in parts:
+                self.s[(self.slot, *at)] = part
+                self.sb[(self.slot, *at)] = part.astype(BF)
 
         every(self.lead, add)
         self.spread(1).start()
@@ -500,8 +506,8 @@
             self.t[self.slot, i] = value
             self.tb[self.slot, i] = value.astype(BF)
 
-        if self.down:
-            every(self.lead[1:], lambda i: put(*i, total(i)))
+        if self.kind != "gate":
+            every((RING,), lambda i: put(*i, total(i)))
         else:
             whole = total(())
             for i in range(RING):
@@ -530,8 +536,8 @@
 
 class Reduces:
     PERIOD = ND + 1 + 2 * NJ + 8
-    START = {"down": 8, "gate": ND + 1 + 3}
-    LAGS = {"down": (0, 3, 4, 7, 8, 12, 14), "gate": (0, 2, 3, 6, 7, 11, 13)}
+    START = {"down": 9, "gate": ND + 1 + 3}
+    LAGS = {"down": (0, 3, 4, 7, 8, 12, 16), "gate": (0, 2, 3, 6, 7, 10, 14)}
 
     def __init__(self, units):
         self.units = units

time: 480 us -> 458 us (0.954)
  Pallas kernels: 465 us -> 443 us
    pallas_call x1, Pallas kernels: 465 us -> 443 us  [call(): pl.pallas_call(kernel, out_shape=(shape(T, D), *outs, *work), in_specs=[h...]
where the time goes in v5:
time: 458 us; the launch traced here: 457 us
  Pallas kernels  443 us (97%)
  local copies, waits for them, and re-layouts  12.7 us (3%)
    pallas_call x1, Pallas kernels, call(): pl.pallas_call(kernel, out_shape=(shape(T, D), *outs, *work), in_specs=[h...  443 us
    unnamed x6, local copies, waits for them, and re-layouts  9.73 us

profile of v5, /device:TPU:0, one launch (start us, length us, event | category | flops | bytes accessed | tf_op | source)
XLA Modules:
  0.0 457.2 jit_solution(10168580285750152925)
XLA Ops:
  0.6 1.1 stack.9
  1.7 1.1 stack.10
  2.8 0.6 dynamic-slice_maximum_fusion
  3.5 0.8 copy.9
  4.3 443.2 %train.1 = (bf16[2048,1280]{1,0:T(8,128)(2,1)}, bf16[2,20,3072]{2,1,0:T(8,128)(2,1)}, bf16[2,20,3072]{2,1,0:T(8,128)(2,1)}, bf16[2,48,1280]{2,1,0:T(8,128)(2,1)}...) custom-call(bf16[2048,1280]{1,0:T(8,128)(2,1)} %bitcast.12, ...), custom_call_target="tpu_custom_call" | custom-call | tf_op jit(solution)/shard_map/train/pallas_call | solution.py:1004
  447.5 0.0 copy-start
  447.5 1.9 copy.10
  449.4 1.9 copy.11
  451.3 5.2 %copy.14 = bf16[1,2048,1280]{2,1,0:T(8,128)(2,1)} copy(bf16[1,2048,1280]{2,1,0:T(8,128)(2,1)} %bitcast.14) | data formatting | bytes 10485760
  456.5 0.0 copy-done
  456.5 0.7 copy.15
Async XLA Ops:
  447.5 9.1 %copy-start = (bf16[2,48,1280]{2,1,0:T(8,128)(2,1)S(1)}, bf16[2,48,1280]{2,1,0:T(8,128)(2,1)}, u32[]{:S(2)}) copy-start(bf16[2,48,1280]{2,1,0:T(8,128)(2,1)} %get-tuple-element.23) | copy-start | bytes 737284

commit v6 on v5

--- a/solution.py
+++ b/solution.py
@@ -194,7 +194,7 @@
     GROUPS = 2 * RINGS + 1
     HALF = D // 2
     CUT = 384
-    TICKS = ((-1, 1, 4, 8, 10, 17, 20, 21), (17, 19, 21, 23, 25, 32, 36, 37))
+    TICKS = ((-1, 1, 6, 8, 10, 17, 20, 21), (17, 19, 21, 23, 25, 32, 36, 37))
 
     def unit(self, l, _):
         self.l, self.slot = l, (l,)
@@ -626,7 +626,7 @@
         gathers.tick(t)
         for part in range(1, len(AlongZ.PARTS) - 1):
 
-            @pl.when(t == min(2 * AlongZ.PARTS[part], gathers.AHEAD) - 1)
+            @pl.when(t == min(2 * AlongZ.PARTS[part], NJ + 1) - 1)
             def _():
                 along_z.finish(part)
 

time: 458 us -> 459 us (level)
  no operation moved by 1% of the time
where the time goes in v6:
time: 459 us; the launch traced here: 458 us
  Pallas kernels  444 us (97%)
  local copies, waits for them, and re-layouts  12.7 us (3%)
    pallas_call x1, Pallas kernels, call(): pl.pallas_call(kernel, out_shape=(shape(T, D), *outs, *work), in_specs=[h...  444 us
    unnamed x6, local copies, waits for them, and re-layouts  9.73 us

profile of v6, /device:TPU:0, one launch (start us, length us, event | category | flops | bytes accessed | tf_op | source)
XLA Modules:
  0.0 458.1 jit_solution(16336751218906514734)
XLA Ops:
  0.6 1.1 stack.9
  1.7 1.1 stack.10
  2.8 0.6 dynamic-slice_maximum_fusion
  3.5 0.8 copy.9
  4.3 444.1 %train.1 = (bf16[2048,1280]{1,0:T(8,128)(2,1)}, bf16[2,20,3072]{2,1,0:T(8,128)(2,1)}, bf16[2,20,3072]{2,1,0:T(8,128)(2,1)}, bf16[2,48,1280]{2,1,0:T(8,128)(2,1)}...) custom-call(bf16[2048,1280]{1,0:T(8,128)(2,1)} %bitcast.12, ...), custom_call_target="tpu_custom_call" | custom-call | tf_op jit(solution)/shard_map/train/pallas_call | solution.py:1004
  448.4 0.0 copy-start
  448.4 1.9 copy.10
  450.3 1.9 copy.11
  452.2 5.2 %copy.14 = bf16[1,2048,1280]{2,1,0:T(8,128)(2,1)} copy(bf16[1,2048,1280]{2,1,0:T(8,128)(2,1)} %bitcast.14) | data formatting | bytes 10485760
  457.4 0.0 copy-done
  457.4 0.7 copy.15
Async XLA Ops:
  448.4 9.1 %copy-start = (bf16[2,48,1280]{2,1,0:T(8,128)(2,1)S(1)}, bf16[2,48,1280]{2,1,0:T(8,128)(2,1)}, u32[]{:S(2)}) copy-start(bf16[2,48,1280]{2,1,0:T(8,128)(2,1)} %get-tuple-element.23) | copy-start | bytes 737284
